TPU v7x, 512 devices: a whole 4x8x8 slice. The times are simulated.
512 devices in a mesh: blk: 64 (over y, z), lay: 8 (over x, core).
Axes of the slice: x: 4, y: 8, z: 8, core: 2. Of those that a mesh axis runs over, the one named last changes fastest.
Arguments:
- matrix_source: float32 [128, 1024, 256], P('lay', 'blk'), may hold values from -6 to 6
- accum: float32 [128, 1024, 256], P('lay', 'blk'), may hold values from 0.02 to 0.5
- faces: float32 [6, 128, 1024, 256], P(None, 'lay', 'blk'), may hold values from 0.03 to 30, as said below
- basis: float32 [4, 128, 1024, 256], P(None, 'lay', 'blk'), may hold values from 0.05 to 0.5
- coarse_diag: float32 [32, 256], P('lay', 'blk'), may hold values from 32 to 128
- coarse_ratio: float32 [4, 32, 256], P(None, 'lay', 'blk'), may hold values from 0.1 to 0.24
- frac_source: float32 [262144], P(('blk', 'lay')), may hold values from -6 to 6
- frac_accum: float32 [262144], P(('blk', 'lay')), may hold values from 0.05 to 0.5
- frac_link: float32 [262144], P(('blk', 'lay')), may hold values from 0.5 to 5
- frac_trans: float32 [2, 262144], P(None, ('blk', 'lay')), may hold values from 0.5 to 5
- frac_cell: int32 [262144], P(('blk', 'lay')), may hold values from 0 to 65535
- frac_peer: int32 [2, 262144], P(None, ('blk', 'lay')), may hold values from 0 to 262143, as said below
- frac_count: int32 [512], P(('blk', 'lay')), may hold values from 1 to 512, as said below
Outputs:
- pressure: float32 [128, 1024, 256], P('lay', 'blk')
- fracture: float32 [262144], P(('blk', 'lay'))
Inputs may be any that keep to these rules, and one draw needn't show every extreme that they name: `faces`: the x+ face of a cell equals the x- face of the next cell along the first dimension, likewise y and z. `frac_count`: some owner has exactly 512 live slots in every draw. `frac_peer`: each entry is a live slot (slot index below its owner's count) of the same owner or of the owner just before or after it in the order blk index * 8 + lay index.
All inputs are finite; a program needn't handle non-finite values.
Results may differ from a plain program's by a relative error of at most 0.0001.
Values sent between devices are 32-bit elements; how exact they have to be, the bound alone decides.
A program may use at most 64 MiB of HBM per device.

v0:
```python
import jax
import jax.numpy as jnp
from jax import lax
from jax.sharding import PartitionSpec as P

BLOCK = 4
ITERS = 2


OMEGA = 0.8


def padded_2(block, sides, width):
    for axis, dim in sides:
        count = lax.axis_size(axis)
        forward = [(i, i + 1) for i in range(count - 1)]
        backward = [(target, source) for source, target in forward]
        low = lax.ppermute(
            lax.slice_in_dim(block, block.shape[dim] - width, None, axis=dim), axis, forward
        )
        high = lax.ppermute(lax.slice_in_dim(block, 0, width, axis=dim), axis, backward)
        block = jnp.concatenate([low, block, high], axis=dim)
    return block


def padded_3(x, sides, width):
    edges = {}
    for axis, dim in sides:
        size, length = (lax.axis_size(axis), x.shape[dim])
        up = [(i, (i + 1) % size) for i in range(size - 1)]
        last = lax.slice_in_dim(x, length - width, length, axis=dim)
        leading = lax.slice_in_dim(x, 0, width, axis=dim)
        edges[dim] = (
            lax.ppermute(last, axis, up),
            lax.ppermute(leading, axis, [(b, a) for a, b in up]),
        )
    done = []
    for _, dim in sides:
        low, high = edges[dim]
        around = [(width, width) if d in done else (0, 0) for d in range(x.ndim)]
        x = jnp.concatenate([jnp.pad(low, around), x, jnp.pad(high, around)], axis=dim)
        done.append(dim)
    return x


def place(block_sums, row_start, col_start):
    return jnp.pad(block_sums, ((row_start, 2 - row_start), (col_start, 2 - col_start)))


def spread(node_terms):
    low_mask = (jnp.arange(BLOCK) < BLOCK // 2).astype(jnp.float32)
    high_mask = 1.0 - low_mask
    x_low = low_mask[None, :, None, None]
    x_high = high_mask[None, :, None, None]
    y_low = low_mask[None, None, None, :]
    y_high = high_mask[None, None, None, :]

    def masked_sum(values, weight):
        return jnp.sum(values * weight, axis=(1, 3))

    spread_sum = place(jnp.sum(node_terms[0], axis=(1, 3)), 1, 1)
    spread_sum = (
        spread_sum
        + place(masked_sum(node_terms[1], x_low), 0, 1)
        + place(masked_sum(node_terms[1], x_high), 2, 1)
    )
    spread_sum = (
        spread_sum
        + place(masked_sum(node_terms[2], y_low), 1, 0)
        + place(masked_sum(node_terms[2], y_high), 1, 2)
    )
    spread_sum = (
        spread_sum
        + place(masked_sum(node_terms[3], x_low * y_low), 0, 0)
        + place(masked_sum(node_terms[3], x_low * y_high), 0, 2)
    )
    spread_sum = (
        spread_sum
        + place(masked_sum(node_terms[3], x_high * y_low), 2, 0)
        + place(masked_sum(node_terms[3], x_high * y_high), 2, 2)
    )
    return spread_sum


def node_values(extended):
    node_rows = extended.shape[0] - 2
    node_cols = extended.shape[1] - 2
    low_mask = jnp.arange(BLOCK) < BLOCK // 2
    x_low = low_mask[None, :, None, None]
    y_low = low_mask[None, None, None, :]

    def node_grid(row_start, col_start):
        return extended[row_start : row_start + node_rows, col_start : col_start + node_cols][
            :, None, :, None
        ]

    full_shape = (node_rows, BLOCK, node_cols, BLOCK)
    centre = jnp.broadcast_to(node_grid(1, 1), full_shape)
    side_x = jnp.broadcast_to(jnp.where(x_low, node_grid(0, 1), node_grid(2, 1)), full_shape)
    side_y = jnp.broadcast_to(jnp.where(y_low, node_grid(1, 0), node_grid(1, 2)), full_shape)
    corner = jnp.where(
        x_low,
        jnp.where(y_low, node_grid(0, 0), node_grid(0, 2)),
        jnp.where(y_low, node_grid(2, 0), node_grid(2, 2)),
    )
    stacked = jnp.stack([centre, side_x, side_y, corner])
    return stacked.reshape(4, node_rows * BLOCK, node_cols * BLOCK)


def prolong(basis, extended):
    fields = node_values(extended)
    return jnp.sum(basis * fields[..., None], axis=0)


def restrict_terms(basis, residual):
    node_sums = jnp.sum(basis * residual[None], axis=3)
    node_rows = node_sums.shape[1] // BLOCK
    node_cols = node_sums.shape[2] // BLOCK
    return spread(node_sums.reshape(4, node_rows, BLOCK, node_cols, BLOCK))


def coarse_second(first_sweep, first_padded, coarse_ratio):
    neighbours = [
        first_padded[:-2, 1:-1],
        first_padded[2:, 1:-1],
        first_padded[1:-1, :-2],
        first_padded[1:-1, 2:],
    ]
    second = first_sweep
    for direction in range(4):
        second = second + coarse_ratio[direction] * neighbours[direction]
    return second


def flow_rows(padded, faces, accum):
    centre = padded[1:-1, 1:-1, 1:-1]
    beside = [
        padded[2:, 1:-1, 1:-1],
        padded[:-2, 1:-1, 1:-1],
        padded[1:-1, 2:, 1:-1],
        padded[1:-1, :-2, 1:-1],
        padded[1:-1, 1:-1, 2:],
        padded[1:-1, 1:-1, :-2],
    ]
    result = accum * centre
    for direction in range(6):
        result = result + faces[direction] * (centre - beside[direction])
    return result


def fetch_rim(pressure):
    return padded_2(pressure, (("blk", 1), ("lay", 0)), 1)


def matrix_rows(pressure_wide, pressure, fracture, faces, accum, cell_index, couple):
    padded = jnp.pad(pressure_wide, ((0, 0), (0, 0), (1, 1)))
    result = flow_rows(padded, faces, accum)
    pressure_at = pressure.reshape(-1)[cell_index]
    link_flux = couple * (pressure_at - fracture)
    linked = jax.ops.segment_sum(link_flux, cell_index, num_segments=pressure.size).reshape(
        pressure.shape
    )
    return (result + linked, pressure_at)


def local(
    matrix_source,
    accum,
    faces,
    basis,
    coarse_diag,
    coarse_ratio,
    frac_source,
    frac_accum,
    frac_link,
    frac_trans,
    frac_cell,
    frac_peer,
    frac_count,
):
    slot_count = frac_source.shape[0]
    cell_rows, cell_cols, depth_cells = matrix_source.shape
    margin = BLOCK // 2
    live_mask = (jnp.arange(slot_count) < frac_count[0]).astype(jnp.float32)
    couple = live_mask * frac_link
    matrix_diag = (
        accum
        + jnp.sum(faces, axis=0)
        + jax.ops.segment_sum(couple, frac_cell, num_segments=accum.size).reshape(accum.shape)
    )
    frac_diag = frac_accum + couple + jnp.sum(frac_trans, axis=0)
    position = lax.axis_index(("blk", "lay"))
    local_peer = frac_peer - (position - 1) * slot_count
    basis_wide = padded_2(basis, (("blk", 2), ("lay", 1)), margin)
    basis_wide = jnp.pad(basis_wide, ((0, 0), (margin, margin), (margin, margin), (0, 0)))
    pressure = jnp.zeros(matrix_source.shape, jnp.float32)
    pressure_wide = jnp.zeros((cell_rows + 2, cell_cols + 2, depth_cells), jnp.float32)
    fracture = jnp.zeros(frac_source.shape, jnp.float32)
    for iteration in range(ITERS):
        if iteration == 0:
            residual = matrix_source
        else:
            pressure_wide = fetch_rim(pressure)
            rows_now, pressure_at = matrix_rows(
                pressure_wide, pressure, fracture, faces, accum, frac_cell, couple
            )
            residual = matrix_source - rows_now
        wide_rows = padded_2(residual, (("blk", 1), ("lay", 0)), margin)
        wide_rows = jnp.pad(wide_rows, ((margin, margin), (margin, margin), (0, 0)))
        extended = restrict_terms(basis_wide, wide_rows)
        first_sweep = extended[2:-2, 2:-2] / coarse_diag
        first_wide = padded_3(first_sweep, (("blk", 1), ("lay", 0)), 1)
        second = coarse_second(first_sweep, first_wide, coarse_ratio)
        node_grid_wide = padded_2(second, (("blk", 1), ("lay", 0)), 1)
        pressure = pressure + prolong(basis, node_grid_wide)
        pressure_wide = fetch_rim(pressure)
        rows_now, pressure_at = matrix_rows(
            pressure_wide, pressure, fracture, faces, accum, frac_cell, couple
        )
        fracture_wide = padded_2(fracture, ((("blk", "lay"), 0),), slot_count)
        peer_values = fracture_wide[local_peer]
        frac_now = (
            frac_accum * fracture
            + couple * (fracture - pressure_at)
            + jnp.sum(frac_trans * (fracture[None] - peer_values), axis=0)
        )
        pressure = pressure + OMEGA * (matrix_source - rows_now) / matrix_diag
        fracture = fracture + OMEGA * live_mask * (frac_source - frac_now) / frac_diag
    return (pressure, fracture)


def solution(mesh):
    return jax.shard_map(
        local,
        mesh=mesh,
        in_specs=(
            P("lay", "blk", None),
            P("lay", "blk", None),
            P(None, "lay", "blk", None),
            P(None, "lay", "blk", None),
            P("lay", "blk"),
            P(None, "lay", "blk"),
            P(("blk", "lay")),
            P(("blk", "lay")),
            P(("blk", "lay")),
            P(None, ("blk", "lay")),
            P(("blk", "lay")),
            P(None, ("blk", "lay")),
            P(("blk", "lay")),
        ),
        out_specs=(P("lay", "blk", None), P(("blk", "lay"))),
        check_vma=False,
    )
```

profile of v0, /device:TPU:33, one launch (start us, length us, event | category | flops | bytes accessed | tf_op | source)
XLA Modules:
  0.0 246.7 jit_solution(10426103249581378936)
XLA Ops:
  0.7 3.8 %collective-permute-start.24 = (f32[512]{0:T(512)S(1)}, f32[512]{0:T(512)S(1)}, u32[]{:S(2)}, u32[]{:S(2)}) collective-permute-start(f32[512]{0:T(512)S(1)} %broadcast.540), channel_id=1, source_target_pairs={{0,1},{1,2},{2,3},{3,4},{4,5},{5,6},{6,7},{7,8},{8,9},{9,10},{10,1... | collective-permute-start | bytes 6152 | tf_op jit(solution)/shard_map/ppermute | solution.py:18
  5.5 4.0 %collective-permute-start.4 = (f32[16,2,256]{2,1,0:T(2,128)S(1)}, f32[16,2,256]{2,1,0:T(2,128)S(1)}, u32[]{:S(2)}, u32[]{:S(2)}) collective-permute-start(f32[16,2,256]{2,1,0:T(2,128)S(1)} %get-tuple-element.50), channel_id=1, source_target_pairs={{0,8},{8,16},{16,24},{24,32},{32,40},{40,48},{48,56},{56,64},{64,7... | collective-permute-start | bytes 98312 | tf_op jit(solution)/shard_map/ppermute | solution.py:18
  9.5 8.5 %collective-permute-start.5 = (f32[16,2,256]{2,1,0:T(2,128)S(1)}, f32[16,2,256]{2,1,0:T(2,128)S(1)}, u32[]{:S(2)}, u32[]{:S(2)}) collective-permute-start(f32[16,2,256]{2,1,0:T(2,128)S(1)} %get-tuple-element.51), channel_id=1, source_target_pairs={{8,0},{16,8},{24,16},{32,24},{40,32},{48,40},{56,48},{64,56},{72,6... | collective-permute-start | bytes 98312 | tf_op jit(solution)/shard_map/ppermute | solution.py:21
  18.0 1.3 fusion.93
  19.3 1.9 collective-permute-start
  21.2 6.7 %collective-permute-start.1 = (f32[4,16,2,256]{3,2,1,0:T(2,128)S(1)}, f32[4,16,2,256]{3,2,1,0:T(2,128)S(1)}, u32[]{:S(2)}, u32[]{:S(2)}) collective-permute-start(f32[4,16,2,256]{3,2,1,0:T(2,128)S(1)} %get-tuple-element.31), channel_id=1, source_target_pairs={{8,0},{16,8},{24,16},{32,24},{40,32},{48,40},{56,48},{64,56},{72,6... | collective-permute-start | bytes 393224 | tf_op jit(solution)/shard_map/ppermute | solution.py:21
  30.8 2.3 reduce_sum.245
  33.1 1.9 collective-permute-start.25
  35.1 3.6 %collective-permute-start.6 = (f32[2,20,256]{2,1,0:T(8,128)S(1)}, f32[2,20,256]{2,1,0:T(8,128)S(1)}, u32[]{:S(2)}, u32[]{:S(2)}) collective-permute-start(f32[2,20,256]{2,1,0:T(8,128)S(1)} %get-tuple-element.34), channel_id=1, source_target_pairs={{0,1},{1,2},{2,3},{3,4},{4,5},{5,6},{6,7},{8,9},{9,10},{10,11},{11... | collective-permute-start | bytes 122888 | tf_op jit(solution)/shard_map/ppermute | solution.py:18
  38.7 1.9 collective-permute-start.7
  40.7 3.6 %collective-permute-start.2 = (f32[4,2,20,256]{3,2,1,0:T(8,128)S(1)}, f32[4,2,20,256]{3,2,1,0:T(8,128)S(1)}, u32[]{:S(2)}, u32[]{:S(2)}) collective-permute-start(f32[4,2,20,256]{3,2,1,0:T(8,128)S(1)} %get-tuple-element.28), channel_id=1, source_target_pairs={{0,1},{1,2},{2,3},{3,4},{4,5},{5,6},{6,7},{8,9},{9,10},{10,11},{11... | collective-permute-start | bytes 491528 | tf_op jit(solution)/shard_map/ppermute | solution.py:18
  44.4 1.9 collective-permute-start.3
  46.4 6.2 %gather_fusion.2 = f32[1024]{0:T(1024)S(1)} fusion(f32[1536]{0:T(1024)S(1)} %pad_maximum_fusion.42, s32[1024]{0:T(1024)S(1)} %broadcast_clamp_fusion), kind=kCustom, calls=%fused_computation.2 | custom fusion | bytes 12288 | tf_op jit(solution)/shard_map/gather | solution.py:221
  54.7 3.6 %collective-permute-start.8 = (f32[1,4]{1,0:T(1,128)S(1)}, f32[1,4]{1,0:T(1,128)S(1)}, u32[]{:S(2)}, u32[]{:S(2)}) collective-permute-start(f32[1,4]{1,0:T(1,128)S(1)} %get-tuple-element.100), channel_id=1, source_target_pairs={{0,1},{1,2},{2,3},{3,4},{4,5},{5,6},{6,7},{8,9},{9,10},{10,11},{11... | collective-permute-start | bytes 56 | tf_op jit(solution)/shard_map/ppermute | solution.py:34
  58.3 1.9 collective-permute-start.11
  60.3 1.9 collective-permute-start.9
  62.2 6.7 %collective-permute-start.10 = (f32[4,1]{1,0:T(4,128)S(1)}, f32[4,1]{1,0:T(4,128)S(1)}, u32[]{:S(2)}, u32[]{:S(2)}) collective-permute-start(f32[4,1]{1,0:T(4,128)S(1)} %get-tuple-element.105), channel_id=1, source_target_pairs={{8,0},{16,8},{24,16},{32,24},{40,32},{48,40},{56,48},{64,56},{72,6... | collective-permute-start | bytes 56 | tf_op jit(solution)/shard_map/ppermute | solution.py:35
  69.9 1.9 collective-permute-start.12
  71.8 6.9 %collective-permute-start.13 = (f32[4,1]{1,0:T(4,128)S(1)}, f32[4,1]{1,0:T(4,128)S(1)}, u32[]{:S(2)}, u32[]{:S(2)}) collective-permute-start(f32[4,1]{1,0:T(4,128)S(1)} %get-tuple-element.99), channel_id=1, source_target_pairs={{8,0},{16,8},{24,16},{32,24},{40,32},{48,40},{56,48},{64,56},{72,6... | collective-permute-start | bytes 56 | tf_op jit(solution)/shard_map/ppermute | solution.py:21
  79.7 2.3 collective-permute-start.15
  82.0 5.5 %collective-permute-start.14 = (f32[1,6]{1,0:T(1,128)S(1)}, f32[1,6]{1,0:T(1,128)S(1)}, u32[]{:S(2)}, u32[]{:S(2)}) collective-permute-start(f32[1,6]{1,0:T(1,128)S(1)} %get-tuple-element.97), channel_id=1, source_target_pairs={{0,1},{1,2},{2,3},{3,4},{4,5},{5,6},{6,7},{8,9},{9,10},{10,11},{11... | collective-permute-start | bytes 80 | tf_op jit(solution)/shard_map/ppermute | solution.py:18
  90.0 1.9 collective-permute-start.16
  91.9 7.2 %collective-permute-start.17 = (f32[16,1,256]{2,1,0:T(1,128)}, f32[16,1,256]{2,1,0:T(1,128)}, u32[]{:S(2)}, u32[]{:S(2)}) collective-permute-start(f32[16,1,256]{2,1,0:T(1,128)} %get-tuple-element.49), channel_id=1, source_target_pairs={{8,0},{16,8},{24,16},{32,24},{40,32},{48,40},{56,48},{64,56},{72,6... | collective-permute-start | bytes 49160 | tf_op jit(solution)/shard_map/ppermute | solution.py:21
  99.9 4.3 %gather_fusion = f32[512]{0:T(512)} fusion(f32[65536]{0:T(1024)S(1)} %bitcast.84, s32[1024]{0:T(1024)S(1)} %copy-done.16), kind=kCustom, calls=%fused_computation | custom fusion | bytes 6144 | tf_op jit(solution)/shard_map/gather | solution.py:158
  104.2 1.4 pad_maximum_fusion.39
  105.6 4.5 %collective-permute-start.19 = (f32[1,18,256]{2,1,0:T(8,128)}, f32[1,18,256]{2,1,0:T(8,128)}, u32[]{:S(2)}, u32[]{:S(2)}) collective-permute-start(f32[1,18,256]{2,1,0:T(8,128)} %get-tuple-element.40), channel_id=1, source_target_pairs={{0,1},{1,2},{2,3},{3,4},{4,5},{5,6},{6,7},{8,9},{9,10},{10,11},{11... | collective-permute-start | bytes 55304 | tf_op jit(solution)/shard_map/ppermute | solution.py:18
  110.1 1.9 collective-permute-start.18
  112.0 1.3 fusion.91
  113.3 3.5 %scatter_custom_fusion = f32[65536]{0:T(1024)S(1)} fusion(s32[512]{0:T(512)} %param.23, f32[512]{0:T(512)} %get-tuple-element.26, f32[]{:T(128)} %constant.13.clone.1), kind=kCustom, calls=%fused_computation.154 | custom fusion | flops 512 | bytes 262656 | tf_op jit(solution)/shard_map/scatter-add | solution.py:160
  117.5 3.5 %scatter_custom_fusion.1 = f32[65536]{0:T(1024)S(1)} fusion(s32[512]{0:T(512)} %param.23, f32[512]{0:T(512)} %get-tuple-element.27, f32[]{:T(128)} %constant.13.clone.1), kind=kCustom, calls=%fused_computation.152 | custom fusion | flops 512 | bytes 262656 | tf_op jit(solution)/shard_map/scatter-add | solution.py:189
  121.8 1.1 select_maximum_fusion.12
  122.9 1.7 fusion.52
  125.3 1.9 collective-permute-start.20
  127.2 6.7 %collective-permute-start.21 = (f32[16,1,256]{2,1,0:T(1,128)}, f32[16,1,256]{2,1,0:T(1,128)}, u32[]{:S(2)}, u32[]{:S(2)}) collective-permute-start(f32[16,1,256]{2,1,0:T(1,128)} %get-tuple-element.47), channel_id=1, source_target_pairs={{8,0},{16,8},{24,16},{32,24},{40,32},{48,40},{56,48},{64,56},{72,6... | collective-permute-start | bytes 49160 | tf_op jit(solution)/shard_map/ppermute | solution.py:21
  134.7 4.4 %gather_fusion.1 = f32[512]{0:T(512)} fusion(f32[65536]{0:T(1024)S(1)} %bitcast.85, s32[1024]{0:T(1024)} %pad_clamp_fusion), kind=kCustom, calls=%fused_computation.1 | custom fusion | bytes 6144 | tf_op jit(solution)/shard_map/gather | solution.py:158
  139.1 1.3 pad_maximum_fusion.36
  140.4 4.2 %collective-permute-start.23 = (f32[1,18,256]{2,1,0:T(8,128)}, f32[1,18,256]{2,1,0:T(8,128)}, u32[]{:S(2)}, u32[]{:S(2)}) collective-permute-start(f32[1,18,256]{2,1,0:T(8,128)} %get-tuple-element.38), channel_id=1, source_target_pairs={{0,1},{1,2},{2,3},{3,4},{4,5},{5,6},{6,7},{8,9},{9,10},{10,11},{11... | collective-permute-start | bytes 55304 | tf_op jit(solution)/shard_map/ppermute | solution.py:18
  144.6 1.9 collective-permute-start.22
  146.5 1.3 subtract_multiply_fusion.1
  147.9 3.5 %scatter_custom_fusion.2 = f32[65536]{0:T(1024)S(1)} fusion(s32[512]{0:T(512)} %param.23, f32[512]{0:T(512)} %get-tuple-element.24, f32[]{:T(128)} %constant.13.clone.1), kind=kCustom, calls=%fused_computation.150 | custom fusion | flops 512 | bytes 262656 | tf_op jit(solution)/shard_map/scatter-add | solution.py:160
  153.3 1.5 fusion.31
  154.8 1.9 collective-permute-start.26
  156.7 6.7 %collective-permute-start.27 = (f32[16,2,256]{2,1,0:T(2,128)S(1)}, f32[16,2,256]{2,1,0:T(2,128)S(1)}, u32[]{:S(2)}, u32[]{:S(2)}) collective-permute-start(f32[16,2,256]{2,1,0:T(2,128)S(1)} %get-tuple-element.45), channel_id=1, source_target_pairs={{8,0},{16,8},{24,16},{32,24},{40,32},{48,40},{56,48},{64,56},{72,6... | collective-permute-start | bytes 98312 | tf_op jit(solution)/shard_map/ppermute | solution.py:21
  163.4 4.2 %collective-permute-start.42 = (f32[512]{0:T(512)S(1)}, f32[512]{0:T(512)S(1)}, u32[]{:S(2)}, u32[]{:S(2)}) collective-permute-start(f32[512]{0:T(512)S(1)} %copy-done.12), channel_id=1, source_target_pairs={{0,1},{1,2},{2,3},{3,4},{4,5},{5,6},{6,7},{7,8},{8,9},{9,10},{10,1... | collective-permute-start | bytes 6152 | tf_op jit(solution)/shard_map/ppermute | solution.py:18
  167.6 1.9 collective-permute-start.43
  170.3 3.6 %collective-permute-start.28 = (f32[2,20,256]{2,1,0:T(8,128)}, f32[2,20,256]{2,1,0:T(8,128)}, u32[]{:S(2)}, u32[]{:S(2)}) collective-permute-start(f32[2,20,256]{2,1,0:T(8,128)} %get-tuple-element.32), channel_id=1, source_target_pairs={{0,1},{1,2},{2,3},{3,4},{4,5},{5,6},{6,7},{8,9},{9,10},{10,11},{11... | collective-permute-start | bytes 122888 | tf_op jit(solution)/shard_map/ppermute | solution.py:18
  173.9 3.9 %collective-permute-start.29 = (f32[2,20,256]{2,1,0:T(8,128)}, f32[2,20,256]{2,1,0:T(8,128)}, u32[]{:S(2)}, u32[]{:S(2)}) collective-permute-start(f32[2,20,256]{2,1,0:T(8,128)} %get-tuple-element.33), channel_id=1, source_target_pairs={{1,0},{2,1},{3,2},{4,3},{5,4},{6,5},{7,6},{9,8},{10,9},{11,10},{12... | collective-permute-start | bytes 122888 | tf_op jit(solution)/shard_map/ppermute | solution.py:21
  177.9 6.3 %gather_fusion.4 = f32[1024]{0:T(1024)S(1)} fusion(f32[1536]{0:T(1024)S(1)} %pad_maximum_fusion.43, s32[1024]{0:T(1024)} %copy-done.11), kind=kCustom, calls=%fused_computation.4 | custom fusion | bytes 12288 | tf_op jit(solution)/shard_map/gather | solution.py:221
  185.3 1.9 multiply_reduce_fusion
  188.3 1.9 collective-permute-start.30
  190.2 2.4 collective-permute-start.33
  192.6 1.9 collective-permute-start.31
  194.6 6.7 %collective-permute-start.32 = (f32[4,1]{1,0:T(4,128)S(1)}, f32[4,1]{1,0:T(4,128)S(1)}, u32[]{:S(2)}, u32[]{:S(2)}) collective-permute-start(f32[4,1]{1,0:T(4,128)S(1)} %get-tuple-element.93), channel_id=1, source_target_pairs={{8,0},{16,8},{24,16},{32,24},{40,32},{48,40},{56,48},{64,56},{72,6... | collective-permute-start | bytes 56 | tf_op jit(solution)/shard_map/ppermute | solution.py:35
  202.3 1.9 collective-permute-start.34
  204.2 6.9 %collective-permute-start.35 = (f32[4,1]{1,0:T(4,128)S(1)}, f32[4,1]{1,0:T(4,128)S(1)}, u32[]{:S(2)}, u32[]{:S(2)}) collective-permute-start(f32[4,1]{1,0:T(4,128)S(1)} %get-tuple-element.87), channel_id=1, source_target_pairs={{8,0},{16,8},{24,16},{32,24},{40,32},{48,40},{56,48},{64,56},{72,6... | collective-permute-start | bytes 56 | tf_op jit(solution)/shard_map/ppermute | solution.py:21
  212.1 3.6 %collective-permute-start.37 = (f32[1,6]{1,0:T(1,128)S(1)}, f32[1,6]{1,0:T(1,128)S(1)}, u32[]{:S(2)}, u32[]{:S(2)}) collective-permute-start(f32[1,6]{1,0:T(1,128)S(1)} %get-tuple-element.84), channel_id=1, source_target_pairs={{1,0},{2,1},{3,2},{4,3},{5,4},{6,5},{7,6},{9,8},{10,9},{11,10},{12... | collective-permute-start | bytes 80 | tf_op jit(solution)/shard_map/ppermute | solution.py:21
  215.7 3.8 %collective-permute-start.36 = (f32[1,6]{1,0:T(1,128)S(1)}, f32[1,6]{1,0:T(1,128)S(1)}, u32[]{:S(2)}, u32[]{:S(2)}) collective-permute-start(f32[1,6]{1,0:T(1,128)S(1)} %get-tuple-element.85), channel_id=1, source_target_pairs={{0,1},{1,2},{2,3},{3,4},{4,5},{5,6},{6,7},{8,9},{9,10},{10,11},{11... | collective-permute-start | bytes 80 | tf_op jit(solution)/shard_map/ppermute | solution.py:18
  221.3 1.9 collective-permute-start.38
  223.3 7.2 %collective-permute-start.39 = (f32[16,1,256]{2,1,0:T(1,128)S(1)}, f32[16,1,256]{2,1,0:T(1,128)S(1)}, u32[]{:S(2)}, u32[]{:S(2)}) collective-permute-start(f32[16,1,256]{2,1,0:T(1,128)S(1)} %get-tuple-element.43), channel_id=1, source_target_pairs={{8,0},{16,8},{24,16},{32,24},{40,32},{48,40},{56,48},{64,56},{72,6... | collective-permute-start | bytes 49160 | tf_op jit(solution)/shard_map/ppermute | solution.py:21
  230.7 3.1 %gather_fusion.3 = f32[512]{0:T(512)S(1)} fusion(f32[65536]{0:T(1024)S(1)} %bitcast.83, s32[1024]{0:T(1024)S(1)} %copy-done.17), kind=kCustom, calls=%fused_computation.3 | custom fusion | bytes 6144 | tf_op jit(solution)/shard_map/gather | solution.py:158
  234.5 4.4 %collective-permute-start.41 = (f32[1,18,256]{2,1,0:T(8,128)}, f32[1,18,256]{2,1,0:T(8,128)S(1)}, u32[]{:S(2)}, u32[]{:S(2)}) collective-permute-start(f32[1,18,256]{2,1,0:T(8,128)} %get-tuple-element.36), channel_id=1, source_target_pairs={{0,1},{1,2},{2,3},{3,4},{4,5},{5,6},{6,7},{8,9},{9,10},{10,11},{11... | collective-permute-start | bytes 55304 | tf_op jit(solution)/shard_map/ppermute | solution.py:18
  239.0 1.9 collective-permute-start.40
  241.6 3.5 %scatter_custom_fusion.3 = f32[65536]{0:T(1024)S(1)} fusion(s32[512]{0:T(512)} %param.23, f32[512]{0:T(512)S(1)} %get-tuple-element.61, f32[]{:T(128)} %constant.13.clone.1), kind=kCustom, calls=%fused_computation.148 | custom fusion | flops 512 | bytes 262656 | tf_op jit(solution)/shard_map/scatter-add | solution.py:160
  245.5 1.2 fusion.13
  (245 shorter events, 23.4 us)
Async XLA Ops:
  0.6 34.4 %copy-start.2 = (f32[16,16,256]{2,1,0:T(8,128)S(1)}, f32[16,16,256]{2,1,0:T(8,128)}, u32[]{:S(2)}) copy-start(f32[16,16,256]{2,1,0:T(8,128)} %param.13) | copy-start | bytes 786436
  0.6 40.0 %copy-start = (f32[4,16,16,256]{3,2,1,0:T(8,128)S(1)}, f32[4,16,16,256]{3,2,1,0:T(8,128)}, u32[]{:S(2)}) copy-start(f32[4,16,16,256]{3,2,1,0:T(8,128)} %param.16) | copy-start | bytes 3145732
  0.7 43.7 %collective-permute-start.24 = (f32[512]{0:T(512)S(1)}, f32[512]{0:T(512)S(1)}, u32[]{:S(2)}, u32[]{:S(2)}) collective-permute-start(f32[512]{0:T(512)S(1)} %broadcast.540), channel_id=1, source_target_pairs={{0,1},{1,2},{2,3},{3,4},{4,5},{5,6},{6,7},{7,8},{8,9},{9,10},{10,1... | collective-permute-start | bytes 6152 | tf_op jit(solution)/shard_map/ppermute | solution.py:18
  5.5 27.6 %collective-permute-start.4 = (f32[16,2,256]{2,1,0:T(2,128)S(1)}, f32[16,2,256]{2,1,0:T(2,128)S(1)}, u32[]{:S(2)}, u32[]{:S(2)}) collective-permute-start(f32[16,2,256]{2,1,0:T(2,128)S(1)} %get-tuple-element.50), channel_id=1, source_target_pairs={{0,8},{8,16},{16,24},{24,32},{32,40},{40,48},{48,56},{56,64},{64,7... | collective-permute-start | bytes 98312 | tf_op jit(solution)/shard_map/ppermute | solution.py:18
  9.5 25.5 %collective-permute-start.5 = (f32[16,2,256]{2,1,0:T(2,128)S(1)}, f32[16,2,256]{2,1,0:T(2,128)S(1)}, u32[]{:S(2)}, u32[]{:S(2)}) collective-permute-start(f32[16,2,256]{2,1,0:T(2,128)S(1)} %get-tuple-element.51), channel_id=1, source_target_pairs={{8,0},{16,8},{24,16},{32,24},{40,32},{48,40},{56,48},{64,56},{72,6... | collective-permute-start | bytes 98312 | tf_op jit(solution)/shard_map/ppermute | solution.py:21
  19.3 19.4 %collective-permute-start = (f32[4,16,2,256]{3,2,1,0:T(2,128)S(1)}, f32[4,16,2,256]{3,2,1,0:T(2,128)S(1)}, u32[]{:S(2)}, u32[]{:S(2)}) collective-permute-start(f32[4,16,2,256]{3,2,1,0:T(2,128)S(1)} %get-tuple-element.30), channel_id=1, source_target_pairs={{0,8},{8,16},{16,24},{24,32},{32,40},{40,48},{48,56},{56,64},{64,7... | collective-permute-start | bytes 393224 | tf_op jit(solution)/shard_map/ppermute | solution.py:18
  21.2 19.4 %collective-permute-start.1 = (f32[4,16,2,256]{3,2,1,0:T(2,128)S(1)}, f32[4,16,2,256]{3,2,1,0:T(2,128)S(1)}, u32[]{:S(2)}, u32[]{:S(2)}) collective-permute-start(f32[4,16,2,256]{3,2,1,0:T(2,128)S(1)} %get-tuple-element.31), channel_id=1, source_target_pairs={{8,0},{16,8},{24,16},{32,24},{40,32},{48,40},{56,48},{64,56},{72,6... | collective-permute-start | bytes 393224 | tf_op jit(solution)/shard_map/ppermute | solution.py:21
  27.9 26.3 %copy-start.26 = (f32[4]{0:T(128)}, f32[4]{0:T(128)S(1)}, u32[]{:S(2)}) copy-start(f32[4]{0:T(128)S(1)} %fusion.88) | copy-start | bytes 52
  27.9 26.3 %copy-start.28 = (f32[4]{0:T(128)}, f32[4]{0:T(128)S(1)}, u32[]{:S(2)}) copy-start(f32[4]{0:T(128)S(1)} %broadcast_subtract_fusion.1) | copy-start | bytes 52
  30.0 24.2 %copy-start.18 = (f32[4,4]{1,0:T(4,128)}, f32[4,4]{1,0:T(4,128)S(1)}, u32[]{:S(2)}) copy-start(f32[4,4]{1,0:T(4,128)S(1)} %get-tuple-element.106) | copy-start | bytes 196
  30.0 24.2 %copy-start.20 = (f32[4,4]{1,0:T(4,128)}, f32[4,4]{1,0:T(4,128)S(1)}, u32[]{:S(2)}) copy-start(f32[4,4]{1,0:T(4,128)S(1)} %get-tuple-element.107) | copy-start | bytes 196
  30.0 24.2 %copy-start.22 = (f32[4,4]{1,0:T(4,128)}, f32[4,4]{1,0:T(4,128)S(1)}, u32[]{:S(2)}) copy-start(f32[4,4]{1,0:T(4,128)S(1)} %get-tuple-element.116) | copy-start | bytes 196
  30.0 24.2 %copy-start.24 = (f32[4,4]{1,0:T(4,128)}, f32[4,4]{1,0:T(4,128)S(1)}, u32[]{:S(2)}) copy-start(f32[4,4]{1,0:T(4,128)S(1)} %get-tuple-element.117) | copy-start | bytes 196
  30.0 58.5 %copy-start.39 = (pred[4]{0:T(512)(128)(4,1)}, pred[4]{0:T(512)(128)(4,1)S(1)}, u32[]{:S(2)}) copy-start(pred[4]{0:T(512)(128)(4,1)S(1)} %iota_compare_fusion.13) | copy-start | bytes 16
  30.8 58.2 %copy-start.41 = (pred[16]{0:T(512)(128)(4,1)}, pred[16]{0:T(512)(128)(4,1)S(1)}, u32[]{:S(2)}) copy-start(pred[16]{0:T(512)(128)(4,1)S(1)} %broadcast_in_dim.249) | copy-start | bytes 52
  33.1 13.2 %collective-permute-start.25 = (f32[512]{0:T(512)S(1)}, f32[512]{0:T(512)S(1)}, u32[]{:S(2)}, u32[]{:S(2)}) collective-permute-start(f32[512]{0:T(512)S(1)} %broadcast.540), channel_id=1, source_target_pairs={{1,0},{2,1},{3,2},{4,3},{5,4},{6,5},{7,6},{8,7},{9,8},{10,9},{11,1... | collective-permute-start | bytes 6152 | tf_op jit(solution)/shard_map/ppermute | solution.py:21
  35.1 17.5 %collective-permute-start.6 = (f32[2,20,256]{2,1,0:T(8,128)S(1)}, f32[2,20,256]{2,1,0:T(8,128)S(1)}, u32[]{:S(2)}, u32[]{:S(2)}) collective-permute-start(f32[2,20,256]{2,1,0:T(8,128)S(1)} %get-tuple-element.34), channel_id=1, source_target_pairs={{0,1},{1,2},{2,3},{3,4},{4,5},{5,6},{6,7},{8,9},{9,10},{10,11},{11... | collective-permute-start | bytes 122888 | tf_op jit(solution)/shard_map/ppermute | solution.py:18
  38.7 13.8 %collective-permute-start.7 = (f32[2,20,256]{2,1,0:T(8,128)S(1)}, f32[2,20,256]{2,1,0:T(8,128)S(1)}, u32[]{:S(2)}, u32[]{:S(2)}) collective-permute-start(f32[2,20,256]{2,1,0:T(8,128)S(1)} %get-tuple-element.35), channel_id=1, source_target_pairs={{1,0},{2,1},{3,2},{4,3},{5,4},{6,5},{7,6},{9,8},{10,9},{11,10},{12... | collective-permute-start | bytes 122888 | tf_op jit(solution)/shard_map/ppermute | solution.py:21
  40.7 12.0 %collective-permute-start.2 = (f32[4,2,20,256]{3,2,1,0:T(8,128)S(1)}, f32[4,2,20,256]{3,2,1,0:T(8,128)S(1)}, u32[]{:S(2)}, u32[]{:S(2)}) collective-permute-start(f32[4,2,20,256]{3,2,1,0:T(8,128)S(1)} %get-tuple-element.28), channel_id=1, source_target_pairs={{0,1},{1,2},{2,3},{3,4},{4,5},{5,6},{6,7},{8,9},{9,10},{10,11},{11... | collective-permute-start | bytes 491528 | tf_op jit(solution)/shard_map/ppermute | solution.py:18
  44.4 8.3 %collective-permute-start.3 = (f32[4,2,20,256]{3,2,1,0:T(8,128)S(1)}, f32[4,2,20,256]{3,2,1,0:T(8,128)S(1)}, u32[]{:S(2)}, u32[]{:S(2)}) collective-permute-start(f32[4,2,20,256]{3,2,1,0:T(8,128)S(1)} %get-tuple-element.29), channel_id=1, source_target_pairs={{1,0},{2,1},{3,2},{4,3},{5,4},{6,5},{7,6},{9,8},{10,9},{11,10},{12... | collective-permute-start | bytes 491528 | tf_op jit(solution)/shard_map/ppermute | solution.py:21
  54.2 45.7 %copy-start.16 = (s32[1024]{0:T(1024)S(1)}, s32[1024]{0:T(1024)}, u32[]{:S(2)}) copy-start(s32[1024]{0:T(1024)} %pad_clamp_fusion) | copy-start | bytes 12292
  54.7 15.0 %collective-permute-start.8 = (f32[1,4]{1,0:T(1,128)S(1)}, f32[1,4]{1,0:T(1,128)S(1)}, u32[]{:S(2)}, u32[]{:S(2)}) collective-permute-start(f32[1,4]{1,0:T(1,128)S(1)} %get-tuple-element.100), channel_id=1, source_target_pairs={{0,1},{1,2},{2,3},{3,4},{4,5},{5,6},{6,7},{8,9},{9,10},{10,11},{11... | collective-permute-start | bytes 56 | tf_op jit(solution)/shard_map/ppermute | solution.py:34
  58.3 11.3 %collective-permute-start.11 = (f32[1,4]{1,0:T(1,128)S(1)}, f32[1,4]{1,0:T(1,128)S(1)}, u32[]{:S(2)}, u32[]{:S(2)}) collective-permute-start(f32[1,4]{1,0:T(1,128)S(1)} %get-tuple-element.101), channel_id=1, source_target_pairs={{1,0},{2,1},{3,2},{4,3},{5,4},{6,5},{7,6},{9,8},{10,9},{11,10},{12... | collective-permute-start | bytes 56 | tf_op jit(solution)/shard_map/ppermute | solution.py:35
  60.3 8.6 %collective-permute-start.9 = (f32[4,1]{1,0:T(4,128)S(1)}, f32[4,1]{1,0:T(4,128)S(1)}, u32[]{:S(2)}, u32[]{:S(2)}) collective-permute-start(f32[4,1]{1,0:T(4,128)S(1)} %get-tuple-element.104), channel_id=1, source_target_pairs={{0,8},{8,16},{16,24},{24,32},{32,40},{40,48},{48,56},{56,64},{64,7... | collective-permute-start | bytes 56 | tf_op jit(solution)/shard_map/ppermute | solution.py:34
  62.2 7.4 %collective-permute-start.10 = (f32[4,1]{1,0:T(4,128)S(1)}, f32[4,1]{1,0:T(4,128)S(1)}, u32[]{:S(2)}, u32[]{:S(2)}) collective-permute-start(f32[4,1]{1,0:T(4,128)S(1)} %get-tuple-element.105), channel_id=1, source_target_pairs={{8,0},{16,8},{24,16},{32,24},{40,32},{48,40},{56,48},{64,56},{72,6... | collective-permute-start | bytes 56 | tf_op jit(solution)/shard_map/ppermute | solution.py:35
  69.9 9.0 %collective-permute-start.12 = (f32[4,1]{1,0:T(4,128)S(1)}, f32[4,1]{1,0:T(4,128)S(1)}, u32[]{:S(2)}, u32[]{:S(2)}) collective-permute-start(f32[4,1]{1,0:T(4,128)S(1)} %get-tuple-element.98), channel_id=1, source_target_pairs={{0,8},{8,16},{16,24},{24,32},{32,40},{40,48},{48,56},{56,64},{64,7... | collective-permute-start | bytes 56 | tf_op jit(solution)/shard_map/ppermute | solution.py:18
  71.8 7.7 %collective-permute-start.13 = (f32[4,1]{1,0:T(4,128)S(1)}, f32[4,1]{1,0:T(4,128)S(1)}, u32[]{:S(2)}, u32[]{:S(2)}) collective-permute-start(f32[4,1]{1,0:T(4,128)S(1)} %get-tuple-element.99), channel_id=1, source_target_pairs={{8,0},{16,8},{24,16},{32,24},{40,32},{48,40},{56,48},{64,56},{72,6... | collective-permute-start | bytes 56 | tf_op jit(solution)/shard_map/ppermute | solution.py:21
  79.7 7.9 %collective-permute-start.15 = (f32[1,6]{1,0:T(1,128)S(1)}, f32[1,6]{1,0:T(1,128)S(1)}, u32[]{:S(2)}, u32[]{:S(2)}) collective-permute-start(f32[1,6]{1,0:T(1,128)S(1)} %get-tuple-element.96), channel_id=1, source_target_pairs={{1,0},{2,1},{3,2},{4,3},{5,4},{6,5},{7,6},{9,8},{10,9},{11,10},{12... | collective-permute-start | bytes 80 | tf_op jit(solution)/shard_map/ppermute | solution.py:21
  82.0 6.2 %collective-permute-start.14 = (f32[1,6]{1,0:T(1,128)S(1)}, f32[1,6]{1,0:T(1,128)S(1)}, u32[]{:S(2)}, u32[]{:S(2)}) collective-permute-start(f32[1,6]{1,0:T(1,128)S(1)} %get-tuple-element.97), channel_id=1, source_target_pairs={{0,1},{1,2},{2,3},{3,4},{4,5},{5,6},{6,7},{8,9},{9,10},{10,11},{11... | collective-permute-start | bytes 80 | tf_op jit(solution)/shard_map/ppermute | solution.py:18
  90.0 14.2 %collective-permute-start.16 = (f32[16,1,256]{2,1,0:T(1,128)}, f32[16,1,256]{2,1,0:T(1,128)S(1)}, u32[]{:S(2)}, u32[]{:S(2)}) collective-permute-start(f32[16,1,256]{2,1,0:T(1,128)} %get-tuple-element.48), channel_id=1, source_target_pairs={{0,8},{8,16},{16,24},{24,32},{32,40},{40,48},{48,56},{56,64},{64,7... | collective-permute-start | bytes 49160 | tf_op jit(solution)/shard_map/ppermute | solution.py:18
  91.9 12.3 %collective-permute-start.17 = (f32[16,1,256]{2,1,0:T(1,128)}, f32[16,1,256]{2,1,0:T(1,128)}, u32[]{:S(2)}, u32[]{:S(2)}) collective-permute-start(f32[16,1,256]{2,1,0:T(1,128)} %get-tuple-element.49), channel_id=1, source_target_pairs={{8,0},{16,8},{24,16},{32,24},{40,32},{48,40},{56,48},{64,56},{72,6... | collective-permute-start | bytes 49160 | tf_op jit(solution)/shard_map/ppermute | solution.py:21
  104.2 18.7 %copy-start.1 = (f32[6,16,16,256]{3,2,1,0:T(8,128)S(1)}, f32[6,16,16,256]{3,2,1,0:T(8,128)}, u32[]{:S(2)}) copy-start(f32[6,16,16,256]{3,2,1,0:T(8,128)} %param.15) | copy-start | bytes 4718596
  105.6 16.2 %collective-permute-start.19 = (f32[1,18,256]{2,1,0:T(8,128)}, f32[1,18,256]{2,1,0:T(8,128)}, u32[]{:S(2)}, u32[]{:S(2)}) collective-permute-start(f32[1,18,256]{2,1,0:T(8,128)} %get-tuple-element.40), channel_id=1, source_target_pairs={{0,1},{1,2},{2,3},{3,4},{4,5},{5,6},{6,7},{8,9},{9,10},{10,11},{11... | collective-permute-start | bytes 55304 | tf_op jit(solution)/shard_map/ppermute | solution.py:18
  110.1 11.7 %collective-permute-start.18 = (f32[1,18,256]{2,1,0:T(8,128)}, f32[1,18,256]{2,1,0:T(8,128)}, u32[]{:S(2)}, u32[]{:S(2)}) collective-permute-start(f32[1,18,256]{2,1,0:T(8,128)} %get-tuple-element.41), channel_id=1, source_target_pairs={{1,0},{2,1},{3,2},{4,3},{5,4},{6,5},{7,6},{9,8},{10,9},{11,10},{12... | collective-permute-start | bytes 55304 | tf_op jit(solution)/shard_map/ppermute | solution.py:21
  125.3 13.8 %collective-permute-start.20 = (f32[16,1,256]{2,1,0:T(1,128)}, f32[16,1,256]{2,1,0:T(1,128)S(1)}, u32[]{:S(2)}, u32[]{:S(2)}) collective-permute-start(f32[16,1,256]{2,1,0:T(1,128)} %get-tuple-element.46), channel_id=1, source_target_pairs={{0,8},{8,16},{16,24},{24,32},{32,40},{40,48},{48,56},{56,64},{64,7... | collective-permute-start | bytes 49160 | tf_op jit(solution)/shard_map/ppermute | solution.py:18
  127.2 11.9 %collective-permute-start.21 = (f32[16,1,256]{2,1,0:T(1,128)}, f32[16,1,256]{2,1,0:T(1,128)}, u32[]{:S(2)}, u32[]{:S(2)}) collective-permute-start(f32[16,1,256]{2,1,0:T(1,128)} %get-tuple-element.47), channel_id=1, source_target_pairs={{8,0},{16,8},{24,16},{32,24},{40,32},{48,40},{56,48},{64,56},{72,6... | collective-permute-start | bytes 49160 | tf_op jit(solution)/shard_map/ppermute | solution.py:21
  140.4 11.7 %collective-permute-start.23 = (f32[1,18,256]{2,1,0:T(8,128)}, f32[1,18,256]{2,1,0:T(8,128)}, u32[]{:S(2)}, u32[]{:S(2)}) collective-permute-start(f32[1,18,256]{2,1,0:T(8,128)} %get-tuple-element.38), channel_id=1, source_target_pairs={{0,1},{1,2},{2,3},{3,4},{4,5},{5,6},{6,7},{8,9},{9,10},{10,11},{11... | collective-permute-start | bytes 55304 | tf_op jit(solution)/shard_map/ppermute | solution.py:18
  144.6 7.5 %collective-permute-start.22 = (f32[1,18,256]{2,1,0:T(8,128)}, f32[1,18,256]{2,1,0:T(8,128)}, u32[]{:S(2)}, u32[]{:S(2)}) collective-permute-start(f32[1,18,256]{2,1,0:T(8,128)} %get-tuple-element.39), channel_id=1, source_target_pairs={{1,0},{2,1},{3,2},{4,3},{5,4},{6,5},{7,6},{9,8},{10,9},{11,10},{12... | collective-permute-start | bytes 55304 | tf_op jit(solution)/shard_map/ppermute | solution.py:21
  154.8 14.8 %collective-permute-start.26 = (f32[16,2,256]{2,1,0:T(2,128)S(1)}, f32[16,2,256]{2,1,0:T(2,128)S(1)}, u32[]{:S(2)}, u32[]{:S(2)}) collective-permute-start(f32[16,2,256]{2,1,0:T(2,128)S(1)} %get-tuple-element.44), channel_id=1, source_target_pairs={{0,8},{8,16},{16,24},{24,32},{32,40},{40,48},{48,56},{56,64},{64,7... | collective-permute-start | bytes 98312 | tf_op jit(solution)/shard_map/ppermute | solution.py:18
  156.7 12.9 %collective-permute-start.27 = (f32[16,2,256]{2,1,0:T(2,128)S(1)}, f32[16,2,256]{2,1,0:T(2,128)S(1)}, u32[]{:S(2)}, u32[]{:S(2)}) collective-permute-start(f32[16,2,256]{2,1,0:T(2,128)S(1)} %get-tuple-element.45), channel_id=1, source_target_pairs={{8,0},{16,8},{24,16},{32,24},{40,32},{48,40},{56,48},{64,56},{72,6... | collective-permute-start | bytes 98312 | tf_op jit(solution)/shard_map/ppermute | solution.py:21
  163.4 14.4 %collective-permute-start.42 = (f32[512]{0:T(512)S(1)}, f32[512]{0:T(512)S(1)}, u32[]{:S(2)}, u32[]{:S(2)}) collective-permute-start(f32[512]{0:T(512)S(1)} %copy-done.12), channel_id=1, source_target_pairs={{0,1},{1,2},{2,3},{3,4},{4,5},{5,6},{6,7},{7,8},{8,9},{9,10},{10,1... | collective-permute-start | bytes 6152 | tf_op jit(solution)/shard_map/ppermute | solution.py:18
  167.6 10.2 %collective-permute-start.43 = (f32[512]{0:T(512)S(1)}, f32[512]{0:T(512)S(1)}, u32[]{:S(2)}, u32[]{:S(2)}) collective-permute-start(f32[512]{0:T(512)S(1)} %copy-done.12), channel_id=1, source_target_pairs={{1,0},{2,1},{3,2},{4,3},{5,4},{6,5},{7,6},{8,7},{9,8},{10,9},{11,1... | collective-permute-start | bytes 6152 | tf_op jit(solution)/shard_map/ppermute | solution.py:21
  170.3 13.9 %collective-permute-start.28 = (f32[2,20,256]{2,1,0:T(8,128)}, f32[2,20,256]{2,1,0:T(8,128)}, u32[]{:S(2)}, u32[]{:S(2)}) collective-permute-start(f32[2,20,256]{2,1,0:T(8,128)} %get-tuple-element.32), channel_id=1, source_target_pairs={{0,1},{1,2},{2,3},{3,4},{4,5},{5,6},{6,7},{8,9},{9,10},{10,11},{11... | collective-permute-start | bytes 122888 | tf_op jit(solution)/shard_map/ppermute | solution.py:18
  173.9 10.3 %collective-permute-start.29 = (f32[2,20,256]{2,1,0:T(8,128)}, f32[2,20,256]{2,1,0:T(8,128)}, u32[]{:S(2)}, u32[]{:S(2)}) collective-permute-start(f32[2,20,256]{2,1,0:T(8,128)} %get-tuple-element.33), channel_id=1, source_target_pairs={{1,0},{2,1},{3,2},{4,3},{5,4},{6,5},{7,6},{9,8},{10,9},{11,10},{12... | collective-permute-start | bytes 122888 | tf_op jit(solution)/shard_map/ppermute | solution.py:21
  185.3 35.1 %copy-start.40 = (pred[4]{0:T(512)(128)(4,1)S(1)}, pred[4]{0:T(512)(128)(4,1)}, u32[]{:S(2)}) copy-start(pred[4]{0:T(512)(128)(4,1)} %copy-done.39) | copy-start | bytes 16
  185.3 35.6 %copy-start.42 = (pred[16]{0:T(512)(128)(4,1)S(1)}, pred[16]{0:T(512)(128)(4,1)}, u32[]{:S(2)}) copy-start(pred[16]{0:T(512)(128)(4,1)} %copy-done.41) | copy-start | bytes 52
  187.9 42.7 %copy-start.13 = (f32[512]{0:T(512)S(1)}, f32[512]{0:T(512)}, u32[]{:S(2)}) copy-start(f32[512]{0:T(512)} %get-tuple-element.25) | copy-start | bytes 6148
  187.9 42.7 %copy-start.33 = (f32[2,512]{1,0:T(2,128)S(1)}, f32[2,512]{1,0:T(2,128)}, u32[]{:S(2)}) copy-start(f32[2,512]{1,0:T(2,128)} %param.22) | copy-start | bytes 12292
  188.3 13.7 %collective-permute-start.30 = (f32[1,4]{1,0:T(1,128)S(1)}, f32[1,4]{1,0:T(1,128)S(1)}, u32[]{:S(2)}, u32[]{:S(2)}) collective-permute-start(f32[1,4]{1,0:T(1,128)S(1)} %get-tuple-element.88), channel_id=1, source_target_pairs={{0,1},{1,2},{2,3},{3,4},{4,5},{5,6},{6,7},{8,9},{9,10},{10,11},{11... | collective-permute-start | bytes 56 | tf_op jit(solution)/shard_map/ppermute | solution.py:34
  190.2 11.8 %collective-permute-start.33 = (f32[1,4]{1,0:T(1,128)S(1)}, f32[1,4]{1,0:T(1,128)S(1)}, u32[]{:S(2)}, u32[]{:S(2)}) collective-permute-start(f32[1,4]{1,0:T(1,128)S(1)} %get-tuple-element.89), channel_id=1, source_target_pairs={{1,0},{2,1},{3,2},{4,3},{5,4},{6,5},{7,6},{9,8},{10,9},{11,10},{12... | collective-permute-start | bytes 56 | tf_op jit(solution)/shard_map/ppermute | solution.py:35
  192.6 8.6 %collective-permute-start.31 = (f32[4,1]{1,0:T(4,128)S(1)}, f32[4,1]{1,0:T(4,128)S(1)}, u32[]{:S(2)}, u32[]{:S(2)}) collective-permute-start(f32[4,1]{1,0:T(4,128)S(1)} %get-tuple-element.92), channel_id=1, source_target_pairs={{0,8},{8,16},{16,24},{24,32},{32,40},{40,48},{48,56},{56,64},{64,7... | collective-permute-start | bytes 56 | tf_op jit(solution)/shard_map/ppermute | solution.py:34
  194.6 7.4 %collective-permute-start.32 = (f32[4,1]{1,0:T(4,128)S(1)}, f32[4,1]{1,0:T(4,128)S(1)}, u32[]{:S(2)}, u32[]{:S(2)}) collective-permute-start(f32[4,1]{1,0:T(4,128)S(1)} %get-tuple-element.93), channel_id=1, source_target_pairs={{8,0},{16,8},{24,16},{32,24},{40,32},{48,40},{56,48},{64,56},{72,6... | collective-permute-start | bytes 56 | tf_op jit(solution)/shard_map/ppermute | solution.py:35
  202.3 9.0 %collective-permute-start.34 = (f32[4,1]{1,0:T(4,128)S(1)}, f32[4,1]{1,0:T(4,128)S(1)}, u32[]{:S(2)}, u32[]{:S(2)}) collective-permute-start(f32[4,1]{1,0:T(4,128)S(1)} %get-tuple-element.86), channel_id=1, source_target_pairs={{0,8},{8,16},{16,24},{24,32},{32,40},{40,48},{48,56},{56,64},{64,7... | collective-permute-start | bytes 56 | tf_op jit(solution)/shard_map/ppermute | solution.py:18
  204.2 7.7 %collective-permute-start.35 = (f32[4,1]{1,0:T(4,128)S(1)}, f32[4,1]{1,0:T(4,128)S(1)}, u32[]{:S(2)}, u32[]{:S(2)}) collective-permute-start(f32[4,1]{1,0:T(4,128)S(1)} %get-tuple-element.87), channel_id=1, source_target_pairs={{8,0},{16,8},{24,16},{32,24},{40,32},{48,40},{56,48},{64,56},{72,6... | collective-permute-start | bytes 56 | tf_op jit(solution)/shard_map/ppermute | solution.py:21
  212.1 7.4 %collective-permute-start.37 = (f32[1,6]{1,0:T(1,128)S(1)}, f32[1,6]{1,0:T(1,128)S(1)}, u32[]{:S(2)}, u32[]{:S(2)}) collective-permute-start(f32[1,6]{1,0:T(1,128)S(1)} %get-tuple-element.84), channel_id=1, source_target_pairs={{1,0},{2,1},{3,2},{4,3},{5,4},{6,5},{7,6},{9,8},{10,9},{11,10},{12... | collective-permute-start | bytes 80 | tf_op jit(solution)/shard_map/ppermute | solution.py:21
  215.7 4.5 %collective-permute-start.36 = (f32[1,6]{1,0:T(1,128)S(1)}, f32[1,6]{1,0:T(1,128)S(1)}, u32[]{:S(2)}, u32[]{:S(2)}) collective-permute-start(f32[1,6]{1,0:T(1,128)S(1)} %get-tuple-element.85), channel_id=1, source_target_pairs={{0,1},{1,2},{2,3},{3,4},{4,5},{5,6},{6,7},{8,9},{9,10},{10,11},{11... | collective-permute-start | bytes 80 | tf_op jit(solution)/shard_map/ppermute | solution.py:18
  221.3 19.6 %copy-start.30 = (f32[512]{0:T(512)S(1)}, f32[512]{0:T(512)}, u32[]{:S(2)}) copy-start(f32[512]{0:T(512)} %get-tuple-element.27) | copy-start | bytes 6148
  221.3 19.6 %copy-start.31 = (f32[512]{0:T(512)S(1)}, f32[512]{0:T(512)}, u32[]{:S(2)}) copy-start(f32[512]{0:T(512)} %get-tuple-element.18) | copy-start | bytes 6148
  221.3 19.6 %copy-start.37 = (f32[512]{0:T(512)S(1)}, f32[512]{0:T(512)}, u32[]{:S(2)}) copy-start(f32[512]{0:T(512)} %param.20) | copy-start | bytes 6148
  221.3 19.6 %copy-start.38 = (f32[512]{0:T(512)S(1)}, f32[512]{0:T(512)}, u32[]{:S(2)}) copy-start(f32[512]{0:T(512)} %param.19) | copy-start | bytes 6148
  221.3 12.5 %collective-permute-start.38 = (f32[16,1,256]{2,1,0:T(1,128)S(1)}, f32[16,1,256]{2,1,0:T(1,128)S(1)}, u32[]{:S(2)}, u32[]{:S(2)}) collective-permute-start(f32[16,1,256]{2,1,0:T(1,128)S(1)} %get-tuple-element.42), channel_id=1, source_target_pairs={{0,8},{8,16},{16,24},{24,32},{32,40},{40,48},{48,56},{56,64},{64,7... | collective-permute-start | bytes 49160 | tf_op jit(solution)/shard_map/ppermute | solution.py:18
  223.3 10.6 %collective-permute-start.39 = (f32[16,1,256]{2,1,0:T(1,128)S(1)}, f32[16,1,256]{2,1,0:T(1,128)S(1)}, u32[]{:S(2)}, u32[]{:S(2)}) collective-permute-start(f32[16,1,256]{2,1,0:T(1,128)S(1)} %get-tuple-element.43), channel_id=1, source_target_pairs={{8,0},{16,8},{24,16},{32,24},{40,32},{48,40},{56,48},{64,56},{72,6... | collective-permute-start | bytes 49160 | tf_op jit(solution)/shard_map/ppermute | solution.py:21
  234.5 10.6 %collective-permute-start.41 = (f32[1,18,256]{2,1,0:T(8,128)}, f32[1,18,256]{2,1,0:T(8,128)S(1)}, u32[]{:S(2)}, u32[]{:S(2)}) collective-permute-start(f32[1,18,256]{2,1,0:T(8,128)} %get-tuple-element.36), channel_id=1, source_target_pairs={{0,1},{1,2},{2,3},{3,4},{4,5},{5,6},{6,7},{8,9},{9,10},{10,11},{11... | collective-permute-start | bytes 55304 | tf_op jit(solution)/shard_map/ppermute | solution.py:18
  239.0 6.1 %collective-permute-start.40 = (f32[1,18,256]{2,1,0:T(8,128)S(1)}, f32[1,18,256]{2,1,0:T(8,128)S(1)}, u32[]{:S(2)}, u32[]{:S(2)}) collective-permute-start(f32[1,18,256]{2,1,0:T(8,128)S(1)} %get-tuple-element.37), channel_id=1, source_target_pairs={{1,0},{2,1},{3,2},{4,3},{5,4},{6,5},{7,6},{9,8},{10,9},{11,10},{12... | collective-permute-start | bytes 55304 | tf_op jit(solution)/shard_map/ppermute | solution.py:21
  (23 other events, 178.8 us)
where the time goes:
time: 249 us; the launch traced here: 247 us
  starting transfers between devices  166 us (67%)
  other arithmetic  39.9 us (16%)
  local copies, waits for them, and re-layouts  34.2 us (14%)
  waiting for transfers between devices  3.99 us (2%)
  between operations  2.83 us (1%)
    ppermute x18, starting transfers between devices, padded_2(): lax.ppermute(lax.slice_in_dim(block, 0, width, axis=dim), axis, backward)  80.1 us
    ppermute x18, starting transfers between devices, padded_2(): lax.ppermute(lax.slice_in_dim(block, block.shape[dim] - width, None, axis...  58.7 us
    ppermute x4, starting transfers between devices, padded_3(): lax.ppermute(leading, axis, [(b, a) for a, b in up])  17.7 us
    gather x3, local copies, waits for them, and re-layouts, local(): peer_values = fracture_wide[local_peer]  12.4 us
    gather x3, local copies, waits for them, and re-layouts, matrix_rows(): pressure_at = pressure.reshape(-1)[cell_index]  11.8 us
    scatter-add x3, other arithmetic, matrix_rows(): jax.ops.segment_sum(link_flux, cell_index, num_segments=pressure.size)  10.4 us
    ppermute x4, starting transfers between devices, padded_3(): lax.ppermute(last, axis, up)  9.39 us
    concatenate x16, other arithmetic, padded_2(): block = jnp.concatenate([low, block, high], axis=dim)  7.5 us
  transfers between devices with their start and end apart: 44, of which 6 were waited for; matrix products, arithmetic and copies ran while one was open for 22% of the time, Pallas kernels for 0%

commit v1 on v0

v1 whole, which is shorter than its diff:
```python
import jax
import jax.numpy as jnp
from jax import lax
from jax.experimental import pallas as pl
from jax.experimental.pallas import tpu as pltpu
from jax.sharding import PartitionSpec as P

MESH = pl.DeviceIdType.MESH
F32 = jnp.float32
BF16 = jnp.bfloat16
I32 = jnp.int32

CX = 16
CY = 16
CZ = 256
FS = 512
OMEGA = 0.8
KEEP = 1.0 - OMEGA
LANES = 128

AROUND = ((-1, -1), (-1, 0), (-1, 1), (0, -1), (0, 1), (1, -1), (1, 0), (1, 1))


def iota(shape, dim):
    return lax.broadcasted_iota(I32, shape, dim)


def lane_sum(v):
    return jnp.sum(v, axis=1, keepdims=True)


def row_sum(v):
    return jnp.sum(v, axis=0, keepdims=True)


def fold(v):
    return v[:, :LANES] + v[:, LANES:]


def split(v):
    high = v.astype(BF16)
    return high, (v - high.astype(F32)).astype(BF16)


def dot(a, b, contract_b):
    return lax.dot_general(a, b, (((1,), (contract_b,)), ((), ())), preferred_element_type=F32)


def kernel(
    n_blk,
    n_lay,
    src_h,
    acc_h,
    fac_h,
    bas_h,
    cd_h,
    cr_h,
    fs_h,
    fa_h,
    fl_h,
    ft_h,
    fc_h,
    fp_h,
    cnt_h,
    out_p,
    out_f,
    src,
    acc,
    fac,
    bas,
    cd,
    cr,
    fsrc,
    facc,
    flink,
    ftrans,
    fcell,
    fpeer,
    cnt,
    P0,
    P1,
    wgt,
    zhot,
    ctile,
    snd,
    rcv,
    bxh,
    byh,
    bys,
    pxh,
    pyh,
    pys,
    fsnd,
    frcv,
    load_sem,
    tile_ssem,
    tile_rsem,
    basis_ssem,
    basis_rsem,
    edge_ssem,
    edge_rsem,
    frac_ssem,
    frac_rsem,
):
    b = lax.axis_index("blk")
    l = lax.axis_index("lay")

    def is_there(step):
        i, j = l + step[0], b + step[1]
        return (i >= 0) & (i < n_lay) & (j >= 0) & (j < n_blk)

    def device(step):
        return (b + step[1], l + step[0])

    position = b * n_lay + l
    has_next = position < n_blk * n_lay - 1
    has_prev = position > 0
    next_dev = ((position + 1) // n_lay, lax.rem(position + 1, n_lay))
    prev_dev = ((position - 1) // n_lay, lax.rem(position - 1 + n_lay, n_lay))

    loads = []
    for i, (hbm, vmem) in enumerate(
        (
            (bas_h, bas),
            (src_h, src),
            (cd_h, cd),
            (cr_h, cr),
            (fc_h, fcell),
            (fl_h, flink),
            (cnt_h, cnt),
            (fac_h, fac),
            (acc_h, acc),
            (fs_h, fsrc),
            (fa_h, facc),
            (ft_h, ftrans),
            (fp_h, fpeer),
        )
    ):
        copy = pltpu.make_async_copy(hbm, vmem, load_sem.at[i])
        copy.start()
        loads.append(copy)

    rcv[...] = jnp.zeros(rcv.shape, F32)
    frcv[...] = jnp.zeros(frcv.shape, F32)
    sides = ((3, 4), (1, 6))
    for s in range(2):
        step_x = AROUND[sides[1][s]]
        step_y = AROUND[sides[0][s]]

        @pl.when(jnp.logical_not(is_there(step_x)))
        def _():
            bxh[s] = jnp.zeros((4, CY, CZ), F32)
            pxh[s] = jnp.zeros((CY, CZ), F32)

        @pl.when(jnp.logical_not(is_there(step_y)))
        def _():
            byh[s] = jnp.zeros((4, CX, CZ), F32)
            pyh[s] = jnp.zeros((CX, CZ), F32)

    barrier = pltpu.get_barrier_semaphore()
    count = jnp.int32(0)
    for step in AROUND:
        there = is_there(step)
        count = count + there.astype(I32)

        @pl.when(there)
        def _():
            pl.semaphore_signal(barrier, inc=1, device_id=device(step), device_id_type=MESH)

    for there, dev in ((has_next, next_dev), (has_prev, prev_dev)):
        count = count + there.astype(I32)

        @pl.when(there)
        def _():
            pl.semaphore_signal(barrier, inc=1, device_id=dev, device_id_type=MESH)

    loads[2].wait()
    loads[3].wait()
    ctile[...] = jnp.zeros(ctile.shape, F32)
    ctile[0, 0:4, 0:4] = cd[...]
    for g in range(4):
        ctile[g + 1, 0:4, 0:4] = cr[g]
    own_static = jnp.zeros((8, LANES), F32)
    for g in range(5):
        own_static = own_static + pltpu.roll(pltpu.roll(ctile[g], 2, axis=0), 8 * g + 2, axis=1)
    snd[0] = own_static

    for s in range(2):
        outer = (15 + 8) if s else 8
        P0[:, outer + (1 if s else -1), :] = jnp.zeros((CX + 2, CZ), F32)
        P1[:, outer + (1 if s else -1), :] = jnp.zeros((CX + 2, CZ), F32)
        P1[17 if s else 0] = jnp.zeros((32, CZ), F32)

    pl.semaphore_wait(barrier, count)

    def tile_copy(kind, i):
        return pltpu.make_async_remote_copy(
            src_ref=snd.at[kind],
            dst_ref=rcv.at[kind, 7 - i],
            send_sem=tile_ssem.at[kind, i],
            recv_sem=tile_rsem.at[kind, 7 - i],
            device_id=device(AROUND[i]),
            device_id_type=MESH,
        )

    def tile_arrival(kind, i):
        return pltpu.make_async_remote_copy(
            src_ref=snd.at[kind],
            dst_ref=rcv.at[kind, i],
            send_sem=tile_ssem.at[kind, i],
            recv_sem=tile_rsem.at[kind, i],
            device_id=device(AROUND[i]),
            device_id_type=MESH,
        )

    def send_tile(kind):
        for i in range(8):

            @pl.when(is_there(AROUND[i]))
            def _():
                tile_copy(kind, i).start()

    def await_tile(kind):
        for i in range(8):

            @pl.when(is_there(AROUND[i]))
            def _():
                tile_arrival(kind, i).wait_recv()

    def side_copy(source, target, ssem, rsem, axis, s, arrival=False):
        slot = s if arrival else 1 - s
        return pltpu.make_async_remote_copy(
            src_ref=source,
            dst_ref=target.at[slot],
            send_sem=ssem.at[axis, s],
            recv_sem=rsem.at[axis, slot],
            device_id=device(AROUND[sides[axis][s]]),
            device_id_type=MESH,
        )

    def basis_copy(axis, s, arrival=False):
        source = bas.at[:, 15 * s] if axis else bys.at[s]
        return side_copy(source, bxh if axis else byh, basis_ssem, basis_rsem, axis, s, arrival)

    def edge_copy(axis, s, arrival=False):
        source = P1.at[16 if s else 1, 8:24] if axis else pys.at[s]
        return side_copy(source, pxh if axis else pyh, edge_ssem, edge_rsem, axis, s, arrival)

    def on_sides(make, axis, act):
        for s in range(2):

            @pl.when(is_there(AROUND[sides[axis][s]]))
            def _():
                act(make(axis, s))

    send_tile(0)

    q = iota((32, LANES), 0)
    lane32 = iota((32, LANES), 1)
    y = lax.rem(q, 16)
    col = jnp.where(q < 16, y // 4 + 2, jnp.where(lax.rem(y, 4) < 2, y // 4 + 1, y // 4 + 3))
    to_col = (lane32 == col).astype(F32)
    sub8 = iota((8, LANES), 0)
    lane8 = iota((8, LANES), 1)
    low_lane = lax.rem(lane8, 8) < 4
    x16 = iota((16, LANES), 0)
    lane16 = iota((16, LANES), 1)
    row_c = x16 // 4 + 2
    row_s = jnp.where(lax.rem(x16, 4) < 2, x16 // 4 + 1, x16 // 4 + 3)
    x_wide = iota((16, CZ), 0)

    def rows_of_half(h):
        return h // 2 + 1, (h // 2 if h % 2 == 0 else h // 2 + 2)

    def pack_rows(row):
        value = jnp.broadcast_to(row(0), (16, CZ))
        for x in range(1, 16):
            value = jnp.where(x_wide == x, jnp.broadcast_to(row(x), (16, CZ)), value)
        return value

    def restrict(residual_row, x_planes, y_planes):
        centre = [None] * 6
        beside = [None] * 6

        def add(into, r, value):
            into[r] = value if into[r] is None else into[r] + value

        for h in range(8):
            first, second = residual_row(2 * h), residual_row(2 * h + 1)
            rc, rs = rows_of_half(h)
            for k, (into, r) in enumerate(((centre, rc), (centre, rs), (beside, rc), (beside, rs))):
                add(into, r, fold(bas[k, 2 * h] * first + bas[k, 2 * h + 1] * second))
        for s, plane in enumerate(x_planes):
            rc, rs = (5, 4) if s else (0, 1)
            for k, (into, r) in enumerate(((centre, rc), (centre, rs), (beside, rc), (beside, rs))):
                add(into, r, fold(bxh[s, k] * plane))
        tile = jnp.zeros((8, LANES), F32)
        y_c = jnp.zeros((16, LANES), F32)
        y_s = jnp.zeros((16, LANES), F32)
        for s, plane in enumerate(y_planes):
            near, far = (5, 6) if s else (2, 1)
            for k in range(4):
                value = lane_sum(fold(byh[s, k] * plane))
                placed = jnp.where(lane16 == (far if k < 2 else near), value, 0.0)
                if k % 2 == 0:
                    y_c = y_c + placed
                else:
                    y_s = y_s + placed
        for r in range(6):
            value = lane_sum(jnp.concatenate([centre[r], beside[r]], axis=0))
            line = row_sum(value * to_col)
            if y_planes:
                line = line + row_sum(
                    jnp.where(row_c == r + 1, y_c, 0.0) + jnp.where(row_s == r + 1, y_s, 0.0)
                )
            tile = tile + jnp.where(sub8 == r + 1, line, 0.0)
        return tile

    def assemble(own, kind):
        tiles = {step: rcv[kind, i] for i, step in enumerate(AROUND)}
        tiles[0, 0] = own
        columns = [
            tiles[0, dj]
            + pltpu.roll(jnp.where(sub8 < 4, tiles[1, dj], tiles[-1, dj]), 4, axis=0)
            for dj in (-1, 0, 1)
        ]
        return (
            columns[1]
            + jnp.where(low_lane, pltpu.roll(columns[0], LANES - 4, axis=1), 0.0)
            + jnp.where(low_lane, 0.0, pltpu.roll(columns[2], 4, axis=1))
        )

    def fields(nodes):
        centre, beside = [], []
        for r in range(6):
            value = lane_sum(jnp.broadcast_to(nodes[r + 1 : r + 2], (32, LANES)) * to_col)
            centre.append(value[:16])
            beside.append(value[16:])
        return centre, beside

    def side_field(nodes):
        centre = jnp.zeros((16, LANES), F32)
        beside = jnp.zeros((16, LANES), F32)
        for r in range(1, 7):
            line = jnp.broadcast_to(nodes[r : r + 1], (16, LANES))
            centre = centre + jnp.where(row_c == r, line, 0.0)
            beside = beside + jnp.where(row_s == r, line, 0.0)
        return centre, beside

    def prolong_row(x, centre, beside):
        rc, rs = rows_of_half(x // 2)
        return (
            bas[0, x] * centre[rc]
            + bas[1, x] * centre[rs]
            + bas[2, x] * beside[rc]
            + bas[3, x] * beside[rs]
        )

    def prolong_x_plane(s, centre, beside):
        rc, rs = (5, 4) if s else (0, 1)
        return (
            bxh[s, 0] * centre[rc]
            + bxh[s, 1] * centre[rs]
            + bxh[s, 2] * beside[rc]
            + bxh[s, 3] * beside[rs]
        )

    def prolong_y_plane(s, nodes):
        centre, beside = side_field(nodes)
        near, far = (5, 6) if s else (2, 1)

        def pick(value, lane):
            return lane_sum(jnp.where(lane16 == lane, value, 0.0))

        return (
            byh[s, 0] * pick(centre, far)
            + byh[s, 1] * pick(beside, far)
            + byh[s, 2] * pick(centre, near)
            + byh[s, 3] * pick(beside, near)
        )

    loads[0].wait()
    on_sides(basis_copy, 1, lambda copy: copy.start())
    for s in range(2):
        for k in range(4):
            bys[s, k] = pack_rows(lambda x: bas[k, x, 15 * s : 15 * s + 1, :])
    on_sides(basis_copy, 0, lambda copy: copy.start())
    loads[1].wait()
    own_part = restrict(lambda x: src[x], (), ())
    snd[1] = own_part
    send_tile(1)

    for i in range(4, 13):
        loads[i].wait()
    cell = fcell[...]
    cell_row = cell // CZ
    cell_z = lax.rem(cell, CZ)
    live = (iota((1, FS), 1) < cnt[...]).astype(F32)
    couple = live * flink[...]
    frac_diag = facc[...] + couple + ftrans[0:1] + ftrans[1:2]
    frac_step = OMEGA * live / frac_diag
    for i in range(4):
        zhot[64 * i : 64 * i + 64] = (iota((64, FS), 0) + 64 * i == cell_z).astype(F32).astype(BF16)

    def gather(plane):
        total = jnp.zeros((1, FS), F32)
        for i in range(4):
            high, low = split(plane(i))
            found = dot(high, zhot[...], 0) + dot(low, zhot[...], 0)
            total = total + row_sum(jnp.where(iota((64, FS), 0) + 64 * i == cell_row, found, 0.0))
        return total

    def scatter(values, put):
        for i in range(4):
            high, low = split(jnp.where(iota((64, FS), 0) + 64 * i == cell_row, values, 0.0))
            found = dot(high, zhot[...], 1) + dot(low, zhot[...], 1)
            put(i, found.reshape(4, CY, CZ))

    def put_diag(i, found):
        for j in range(4):
            x = 4 * i + j
            total = found[j] + acc[x]
            for d in range(6):
                total = total + fac[d, x]
            acc[x] = total
            wgt[x] = OMEGA / total

    scatter(couple, put_diag)
    lane_z = iota((16, CZ), 1)
    for x in range(16):
        fac[4, x] = jnp.where(lane_z == CZ - 1, 0.0, fac[4, x])
        fac[5, x] = jnp.where(lane_z == 0, 0.0, fac[5, x])
    edge_face = [
        pack_rows(lambda x: fac[3, x, 0:1, :]),
        pack_rows(lambda x: fac[2, x, 15:16, :]),
    ]

    await_tile(0)
    coarse = assemble(own_static, 0)
    in_group = lane8 < 8
    diag = jnp.where(in_group, coarse, 0.0)
    inverse = jnp.where(diag > 0.0, 1.0 / jnp.where(diag > 0.0, diag, 1.0), 0.0)
    ratio = [
        jnp.where(in_group, pltpu.roll(coarse, LANES - 8 * (g + 1), axis=1), 0.0) for g in range(4)
    ]

    def coarse_solve(own, kind):
        await_tile(kind)
        first = assemble(own, kind) * inverse
        return (
            first
            + ratio[0] * pltpu.roll(first, 1, axis=0)
            + ratio[1] * pltpu.roll(first, 7, axis=0)
            + ratio[2] * pltpu.roll(first, 1, axis=1)
            + ratio[3] * pltpu.roll(first, LANES - 1, axis=1)
        )

    def off_diagonal(p, x):
        middle = p[x + 1, 8:24]
        return (
            fac[0, x] * p[x + 2, 8:24]
            + fac[1, x] * p[x, 8:24]
            + fac[2, x] * p[x + 1, 9:25]
            + fac[3, x] * p[x + 1, 7:23]
            + fac[4, x] * pltpu.roll(middle, CZ - 1, axis=1)
            + fac[5, x] * pltpu.roll(middle, 1, axis=1)
        )

    def own_rows(p, i):
        return p[4 * i + 1 : 4 * i + 5, 8:24].reshape(64, CZ)

    nodes = coarse_solve(own_part, 1)
    centre, beside = fields(nodes)
    for x in range(16):
        P0[x + 1, 8:24] = prolong_row(x, centre, beside)
    frac_now = frac_step * (fsrc[...] + couple * gather(lambda i: own_rows(P0, i)))
    for t in range(4):
        fsnd[t : t + 1, :] = frac_now[:, LANES * t : LANES * t + LANES]

    def frac_copy(s, arrival=False):
        slot = s if arrival else 1 - s
        return pltpu.make_async_remote_copy(
            src_ref=fsnd,
            dst_ref=frcv.at[slot],
            send_sem=frac_ssem.at[s],
            recv_sem=frac_rsem.at[slot],
            device_id=next_dev if s else prev_dev,
            device_id_type=MESH,
        )

    def on_owners(act):
        for s, there in enumerate((has_prev, has_next)):

            @pl.when(there)
            def _():
                act(s)

    on_owners(lambda s: frac_copy(s).start())

    on_sides(lambda axis, s: basis_copy(axis, s, True), 1, lambda copy: copy.wait_recv())
    on_sides(lambda axis, s: basis_copy(axis, s, True), 0, lambda copy: copy.wait_recv())

    def set_rims(p, earlier):
        for s in range(2):
            plane = prolong_x_plane(s, centre, beside)
            p[17 if s else 0, 8:24] = plane + pxh[s] if earlier else plane
            plane = prolong_y_plane(s, nodes)
            if earlier:
                plane = plane + pyh[s]
            for x in range(16):
                p[x + 1, 24 if s else 7, :] = plane[x]

    set_rims(P0, False)
    for x in range(16):
        P1[x + 1, 8:24] = KEEP * P0[x + 1, 8:24] + wgt[x] * (src[x] + off_diagonal(P0, x))
    on_sides(edge_copy, 1, lambda copy: copy.start())
    for s in range(2):
        pys[s] = pack_rows(lambda x: P1[x + 1, 8 + 15 * s : 9 + 15 * s, :])
    on_sides(edge_copy, 0, lambda copy: copy.start())

    def put_source(i, found):
        for j in range(4):
            src[4 * i + j] = src[4 * i + j] + found[j]

    scatter(couple * frac_now, put_source)
    own_part = restrict(
        lambda x: src[x] - acc[x] * P1[x + 1, 8:24] + off_diagonal(P1, x),
        (fac[1, 0] * P1[1, 8:24], fac[0, 15] * P1[16, 8:24]),
        (edge_face[0] * pys[0], edge_face[1] * pys[1]),
    )
    snd[2] = own_part
    send_tile(2)

    nodes = coarse_solve(own_part, 2)
    centre, beside = fields(nodes)
    for x in range(16):
        P0[x + 1, 8:24] = P1[x + 1, 8:24] + prolong_row(x, centre, beside)
    on_sides(lambda axis, s: edge_copy(axis, s, True), 1, lambda copy: copy.wait_recv())
    on_sides(lambda axis, s: edge_copy(axis, s, True), 0, lambda copy: copy.wait_recv())
    set_rims(P0, True)
    for x in range(16):
        out_p[x] = KEEP * P0[x + 1, 8:24] + wgt[x] * (src[x] + off_diagonal(P0, x))

    pressure_at = gather(lambda i: own_rows(P0, i))
    on_owners(lambda s: frac_copy(s, True).wait_recv())
    table = jnp.concatenate([frcv[0], fsnd[...], frcv[1], jnp.zeros((4, LANES), F32)], axis=0)
    high, low = split(table)
    peers = jnp.zeros((1, FS), F32)
    for j in range(2):
        local = fpeer[j : j + 1] - (position - 1) * FS
        hot = (iota((LANES, FS), 0) == lax.rem(local, LANES)).astype(F32).astype(BF16)
        found = dot(high, hot, 0) + dot(low, hot, 0)
        peers = peers + ftrans[j : j + 1] * row_sum(
            jnp.where(iota((16, FS), 0) == local // LANES, found, 0.0)
        )
    out_f[...] = frac_now + frac_step * (
        fsrc[...] + couple * pressure_at + peers - frac_diag * frac_now
    )

    for kind in range(3):
        for i in range(8):

            @pl.when(is_there(AROUND[i]))
            def _():
                tile_copy(kind, i).wait_send()

    for axis in range(2):
        on_sides(basis_copy, axis, lambda copy: copy.wait_send())
        on_sides(edge_copy, axis, lambda copy: copy.wait_send())
    on_owners(lambda s: frac_copy(s).wait_send())


def solution(mesh):
    n_blk, n_lay = mesh.shape["blk"], mesh.shape["lay"]

    def local(src, acc, fac, bas, cd, cr, fs, fa, fl, ft, fc, fp, cnt):
        row = lambda v: v.reshape(1, v.shape[0])
        operands = (src, acc, fac, bas, cd, cr, row(fs), row(fa), row(fl), ft, row(fc), fp, row(cnt))
        vmem = pltpu.VMEM
        pressure, fracture = pl.pallas_call(
            lambda *refs: kernel(n_blk, n_lay, *refs),
            out_shape=(
                jax.ShapeDtypeStruct((CX, CY, CZ), F32),
                jax.ShapeDtypeStruct((1, FS), F32),
            ),
            in_specs=[pl.BlockSpec(memory_space=pl.ANY)] * 13,
            out_specs=[pl.BlockSpec(memory_space=vmem)] * 2,
            scratch_shapes=[vmem(v.shape, v.dtype) for v in operands]
            + [
                vmem((CX + 2, 32, CZ), F32),
                vmem((CX + 2, 32, CZ), F32),
                vmem((CX, CY, CZ), F32),
                vmem((CZ, FS), BF16),
                vmem((5, 8, LANES), F32),
                vmem((3, 8, LANES), F32),
                vmem((3, 8, 8, LANES), F32),
                vmem((2, 4, CY, CZ), F32),
                vmem((2, 4, CX, CZ), F32),
                vmem((2, 4, CX, CZ), F32),
                vmem((2, CY, CZ), F32),
                vmem((2, CX, CZ), F32),
                vmem((2, CX, CZ), F32),
                vmem((4, LANES), F32),
                vmem((2, 4, LANES), F32),
                pltpu.SemaphoreType.DMA((13,)),
                pltpu.SemaphoreType.DMA((3, 8)),
                pltpu.SemaphoreType.DMA((3, 8)),
                pltpu.SemaphoreType.DMA((2, 2)),
                pltpu.SemaphoreType.DMA((2, 2)),
                pltpu.SemaphoreType.DMA((2, 2)),
                pltpu.SemaphoreType.DMA((2, 2)),
                pltpu.SemaphoreType.DMA((2,)),
                pltpu.SemaphoreType.DMA((2,)),
            ],
            compiler_params=pltpu.CompilerParams(collective_id=0, has_side_effects=True),
        )(*operands)
        return pressure, fracture.reshape(FS)

    return jax.shard_map(
        local,
        mesh=mesh,
        in_specs=(
            P("lay", "blk", None),
            P("lay", "blk", None),
            P(None, "lay", "blk", None),
            P(None, "lay", "blk", None),
            P("lay", "blk"),
            P(None, "lay", "blk"),
            P(("blk", "lay")),
            P(("blk", "lay")),
            P(("blk", "lay")),
            P(None, ("blk", "lay")),
            P(("blk", "lay")),
            P(None, ("blk", "lay")),
            P(("blk", "lay")),
        ),
        out_specs=(P("lay", "blk", None), P(("blk", "lay"))),
        check_vma=False,
    )
```

time: 249 us -> 30.1 us (0.12)
  starting transfers between devices: 166 us -> 0 us
  other arithmetic: 39.9 us -> 0 us
  local copies, waits for them, and re-layouts: 34.2 us -> 2.92 us
  Pallas kernels: 0 us -> 25.7 us
  waiting for transfers between devices: 3.99 us -> 0 us
    ppermute x44 -> x0, starting transfers between devices: 166 us -> none  [the longest x18 80.1 us: padded_2(): lax.ppermute(lax.slice_in_dim(block, 0, width, axis=dim), axis, backward)]
    pallas_call x0 -> x1, Pallas kernels: none -> 25.7 us  [local(): pl.pallas_call(lambda *refs: kernel(n_blk, n_lay, *refs), out_shape=(jax....]
    gather x6 -> x0, local copies, waits for them, and re-layouts: 24.3 us -> none  [the longest x3 12.4 us: local(): peer_values = fracture_wide[local_peer]]
    scatter-add x4 -> x0, other arithmetic: 13.9 us -> none  [the longest x3 10.4 us: matrix_rows(): jax.ops.segment_sum(link_flux, cell_index, num_segments=pressure.size)]
    concatenate x20 -> x0, other arithmetic: 7.8 us -> none  [the longest x16 7.5 us: padded_2(): block = jnp.concatenate([low, block, high], axis=dim)]
    reduce_sum x12 -> x0, other arithmetic: 6.85 us -> none  [the longest x2 2.86 us: restrict_terms(): node_sums = jnp.sum(basis * residual[None], axis=3)]
    slice x22 -> x0, local copies, waits for them, and re-layouts: 4.39 us -> none  [the longest x8 3.77 us: padded_2(): lax.slice_in_dim(block, block.shape[dim] - width, None, axis=dim)]
    ppermute x44 -> x0, waiting for transfers between devices: 3.99 us -> none  [the longest x18 1.42 us: padded_2(): lax.ppermute(lax.slice_in_dim(block, block.shape[dim] - width, None, axis...]
  transfers between devices with their start and end apart: 44 -> 0, of which waited for: 6 -> 0; matrix products, arithmetic and copies ran while one was open for 22% -> 0% of each run, Pallas kernels for 0% -> 0%
where the time goes in v1:
time: 30.1 us; the launch traced here: 29.9 us
  Pallas kernels  25.7 us (85%)
  local copies, waits for them, and re-layouts  2.92 us (10%)
  between operations  1.29 us (4%)
    pallas_call x1, Pallas kernels, local(): pl.pallas_call(lambda *refs: kernel(n_blk, n_lay, *refs), out_shape=(jax....  25.7 us
    unnamed x2, local copies, waits for them, and re-layouts  2.92 us

profile of v1, /device:TPU:33, one launch (start us, length us, event | category | flops | bytes accessed | tf_op | source)
XLA Modules:
  0.0 29.9 jit_solution(11302642230168802714)
XLA Ops:
  1.3 25.7 %shard_map.140 = (f32[16,16,256]{2,1,0:T(8,128)}, f32[1,512]{1,0:T(1,128)}) custom-call(f32[16,16,256]{2,1,0:T(8,128)} %refs_0_.1, f32[16,16,256]{2,1,0:T(8,128)} %refs_1_.1, f32[6,16,16,256]{3,2,1,0:T(8,128)} %refs_2_.1, f32[4,16,16,256]{3,2,1,0:T(8,128)} %refs_3_.1, f32[4,4]{1,0:T(4,128)} %refs_4_.1, f32[4,4,4]{2,1,0:T(4,128)} %refs_5_.1, ...), custom_call_target="tpu_custom_call" | custom-call | tf_op jit(solution)/shard_map/pallas_call | solution.py:580
  27.0 1.7 %copy.18 = f32[16,16,256]{2,1,0:T(8,128)} copy(f32[16,16,256]{2,1,0:T(8,128)} %get-tuple-element.8) | data formatting | bytes 524288
  28.6 1.2 %copy.19 = f32[512]{0:T(512)} copy(f32[512]{0:T(512)} %bitcast.11) | data formatting | bytes 4096

commit v2 on v1

--- a/solution.py
+++ b/solution.py
@@ -81,6 +81,8 @@
     P1,
     wgt,
     zhot,
+    chot,
+    near,
     ctile,
     snd,
     rcv,
@@ -127,7 +129,6 @@
             (cr_h, cr),
             (fc_h, fcell),
             (fl_h, flink),
-            (cnt_h, cnt),
             (fac_h, fac),
             (acc_h, acc),
             (fs_h, fsrc),
@@ -137,25 +138,9 @@
         )
     ):
         copy = pltpu.make_async_copy(hbm, vmem, load_sem.at[i])
-        copy.start()
+        if i < 2:
+            copy.start()
         loads.append(copy)
-
-    rcv[...] = jnp.zeros(rcv.shape, F32)
-    frcv[...] = jnp.zeros(frcv.shape, F32)
-    sides = ((3, 4), (1, 6))
-    for s in range(2):
-        step_x = AROUND[sides[1][s]]
-        step_y = AROUND[sides[0][s]]
-
-        @pl.when(jnp.logical_not(is_there(step_x)))
-        def _():
-            bxh[s] = jnp.zeros((4, CY, CZ), F32)
-            pxh[s] = jnp.zeros((CY, CZ), F32)
-
-        @pl.when(jnp.logical_not(is_there(step_y)))
-        def _():
-            byh[s] = jnp.zeros((4, CX, CZ), F32)
-            pyh[s] = jnp.zeros((CX, CZ), F32)
 
     barrier = pltpu.get_barrier_semaphore()
     count = jnp.int32(0)
@@ -173,6 +158,37 @@
         @pl.when(there)
         def _():
             pl.semaphore_signal(barrier, inc=1, device_id=dev, device_id_type=MESH)
+
+    for i in range(2, len(loads)):
+        loads[i].start()
+
+    sides = ((3, 4), (1, 6))
+    for i, step in enumerate(AROUND):
+
+        @pl.when(jnp.logical_not(is_there(step)))
+        def _():
+            for kind in range(2):
+                rcv[kind, i] = jnp.zeros((8, LANES), F32)
+
+    for s, there in enumerate((has_prev, has_next)):
+
+        @pl.when(jnp.logical_not(there))
+        def _():
+            frcv[s] = jnp.zeros((4, LANES), F32)
+
+    for s in range(2):
+        step_x = AROUND[sides[1][s]]
+        step_y = AROUND[sides[0][s]]
+
+        @pl.when(jnp.logical_not(is_there(step_x)))
+        def _():
+            bxh[s] = jnp.zeros((4, CY, CZ), F32)
+            pxh[s] = jnp.zeros((CY, CZ), F32)
+
+        @pl.when(jnp.logical_not(is_there(step_y)))
+        def _():
+            byh[s] = jnp.zeros((4, CX, CZ), F32)
+            pyh[s] = jnp.zeros((CX, CZ), F32)
 
     loads[2].wait()
     loads[3].wait()
@@ -183,15 +199,12 @@
     own_static = jnp.zeros((8, LANES), F32)
     for g in range(5):
         own_static = own_static + pltpu.roll(pltpu.roll(ctile[g], 2, axis=0), 8 * g + 2, axis=1)
-    snd[0] = own_static
 
     for s in range(2):
         outer = (15 + 8) if s else 8
         P0[:, outer + (1 if s else -1), :] = jnp.zeros((CX + 2, CZ), F32)
         P1[:, outer + (1 if s else -1), :] = jnp.zeros((CX + 2, CZ), F32)
         P1[17 if s else 0] = jnp.zeros((32, CZ), F32)
-
-    pl.semaphore_wait(barrier, count)
 
     def tile_copy(kind, i):
         return pltpu.make_async_remote_copy(
@@ -252,8 +265,6 @@
             @pl.when(is_there(AROUND[sides[axis][s]]))
             def _():
                 act(make(axis, s))
-
-    send_tile(0)
 
     q = iota((32, LANES), 0)
     lane32 = iota((32, LANES), 1)
@@ -380,22 +391,23 @@
         )
 
     loads[0].wait()
-    on_sides(basis_copy, 1, lambda copy: copy.start())
+    loads[1].wait()
+    own_tile = own_static + pltpu.roll(restrict(lambda x: src[x], (), ()), 40, axis=1)
+    snd[0] = own_tile
     for s in range(2):
         for k in range(4):
             bys[s, k] = pack_rows(lambda x: bas[k, x, 15 * s : 15 * s + 1, :])
+    pl.semaphore_wait(barrier, count)
+    send_tile(0)
     on_sides(basis_copy, 0, lambda copy: copy.start())
-    loads[1].wait()
-    own_part = restrict(lambda x: src[x], (), ())
-    snd[1] = own_part
-    send_tile(1)
-
-    for i in range(4, 13):
+    on_sides(basis_copy, 1, lambda copy: copy.start())
+
+    for i in range(4, 12):
         loads[i].wait()
     cell = fcell[...]
     cell_row = cell // CZ
     cell_z = lax.rem(cell, CZ)
-    live = (iota((1, FS), 1) < cnt[...]).astype(F32)
+    live = (iota((1, FS), 1) < cnt_h[0]).astype(F32)
     couple = live * flink[...]
     frac_diag = facc[...] + couple + ftrans[0:1] + ftrans[1:2]
     frac_step = OMEGA * live / frac_diag
@@ -415,6 +427,37 @@
             high, low = split(jnp.where(iota((64, FS), 0) + 64 * i == cell_row, values, 0.0))
             found = dot(high, zhot[...], 1) + dot(low, zhot[...], 1)
             put(i, found.reshape(4, CY, CZ))
+
+    slot_x = cell // (CY * CZ)
+    slot_y = lax.rem(cell_row, CY)
+
+    def node_of(v):
+        return v // 4 + 2, jnp.where(lax.rem(v, 4) < 2, v // 4 + 1, v // 4 + 3)
+
+    slot_rows = node_of(slot_x)
+    slot_cols = node_of(slot_y)
+    for i in range(2):
+        chot[i] = (iota((LANES, FS), 0) == slot_cols[i]).astype(F32).astype(BF16)
+    at_slot = [gather(lambda i: bas[k, 4 * i : 4 * i + 4].reshape(64, CZ)) for k in range(4)]
+    sub_slot = iota((8, FS), 0)
+    for i in range(2):
+        near[i] = jnp.where(sub_slot == slot_rows[0], at_slot[2 * i], 0.0) + jnp.where(
+            sub_slot == slot_rows[1], at_slot[2 * i + 1], 0.0
+        )
+
+    def prolong_at_slots(nodes):
+        high, low = split(nodes)
+        return row_sum(
+            near[0] * (dot(high, chot[0], 0) + dot(low, chot[0], 0))
+            + near[1] * (dot(high, chot[1], 0) + dot(low, chot[1], 0))
+        )
+
+    def restrict_from_slots(values):
+        total = jnp.zeros((8, LANES), F32)
+        for i in range(2):
+            high, low = split(near[i] * values)
+            total = total + dot(high, chot[i], 1) + dot(low, chot[i], 1)
+        return total
 
     def put_diag(i, found):
         for j in range(4):
@@ -435,18 +478,14 @@
         pack_rows(lambda x: fac[2, x, 15:16, :]),
     ]
 
-    await_tile(0)
-    coarse = assemble(own_static, 0)
     in_group = lane8 < 8
-    diag = jnp.where(in_group, coarse, 0.0)
-    inverse = jnp.where(diag > 0.0, 1.0 / jnp.where(diag > 0.0, diag, 1.0), 0.0)
-    ratio = [
-        jnp.where(in_group, pltpu.roll(coarse, LANES - 8 * (g + 1), axis=1), 0.0) for g in range(4)
-    ]
-
-    def coarse_solve(own, kind):
-        await_tile(kind)
-        first = assemble(own, kind) * inverse
+
+    def group(window, g):
+        moved = pltpu.roll(window, LANES - 8 * g, axis=1) if g else window
+        return jnp.where(in_group, moved, 0.0)
+
+    def coarse_solve(rhs):
+        first = rhs * inverse
         return (
             first
             + ratio[0] * pltpu.roll(first, 1, axis=0)
@@ -469,11 +508,16 @@
     def own_rows(p, i):
         return p[4 * i + 1 : 4 * i + 5, 8:24].reshape(64, CZ)
 
-    nodes = coarse_solve(own_part, 1)
+    await_tile(0)
+    window = assemble(own_tile, 0)
+    diag = group(window, 0)
+    inverse = jnp.where(diag > 0.0, 1.0 / jnp.where(diag > 0.0, diag, 1.0), 0.0)
+    ratio = [group(window, g + 1) for g in range(4)]
+    nodes = coarse_solve(group(window, 5))
     centre, beside = fields(nodes)
     for x in range(16):
         P0[x + 1, 8:24] = prolong_row(x, centre, beside)
-    frac_now = frac_step * (fsrc[...] + couple * gather(lambda i: own_rows(P0, i)))
+    frac_now = frac_step * (fsrc[...] + couple * prolong_at_slots(nodes))
     for t in range(4):
         fsnd[t : t + 1, :] = frac_now[:, LANES * t : LANES * t + LANES]
 
@@ -518,30 +562,20 @@
         pys[s] = pack_rows(lambda x: P1[x + 1, 8 + 15 * s : 9 + 15 * s, :])
     on_sides(edge_copy, 0, lambda copy: copy.start())
 
-    def put_source(i, found):
-        for j in range(4):
-            src[4 * i + j] = src[4 * i + j] + found[j]
-
-    scatter(couple * frac_now, put_source)
-    own_part = restrict(
+    own_part = restrict_from_slots(couple * frac_now) + restrict(
         lambda x: src[x] - acc[x] * P1[x + 1, 8:24] + off_diagonal(P1, x),
         (fac[1, 0] * P1[1, 8:24], fac[0, 15] * P1[16, 8:24]),
         (edge_face[0] * pys[0], edge_face[1] * pys[1]),
     )
-    snd[2] = own_part
-    send_tile(2)
-
-    nodes = coarse_solve(own_part, 2)
-    centre, beside = fields(nodes)
-    for x in range(16):
-        P0[x + 1, 8:24] = P1[x + 1, 8:24] + prolong_row(x, centre, beside)
-    on_sides(lambda axis, s: edge_copy(axis, s, True), 1, lambda copy: copy.wait_recv())
-    on_sides(lambda axis, s: edge_copy(axis, s, True), 0, lambda copy: copy.wait_recv())
-    set_rims(P0, True)
-    for x in range(16):
-        out_p[x] = KEEP * P0[x + 1, 8:24] + wgt[x] * (src[x] + off_diagonal(P0, x))
-
-    pressure_at = gather(lambda i: own_rows(P0, i))
+    snd[1] = own_part
+    send_tile(1)
+
+    def put_source(i, found):
+        for j in range(4):
+            src[4 * i + j] = src[4 * i + j] + found[j]
+
+    scatter(couple * frac_now, put_source)
+    pressure_at = gather(lambda i: own_rows(P1, i))
     on_owners(lambda s: frac_copy(s, True).wait_recv())
     table = jnp.concatenate([frcv[0], fsnd[...], frcv[1], jnp.zeros((4, LANES), F32)], axis=0)
     high, low = split(table)
@@ -553,11 +587,23 @@
         peers = peers + ftrans[j : j + 1] * row_sum(
             jnp.where(iota((16, FS), 0) == local // LANES, found, 0.0)
         )
+
+    await_tile(1)
+    nodes = coarse_solve(assemble(own_part, 1))
+    centre, beside = fields(nodes)
+    for x in range(16):
+        P0[x + 1, 8:24] = P1[x + 1, 8:24] + prolong_row(x, centre, beside)
+    on_sides(lambda axis, s: edge_copy(axis, s, True), 1, lambda copy: copy.wait_recv())
+    on_sides(lambda axis, s: edge_copy(axis, s, True), 0, lambda copy: copy.wait_recv())
+    set_rims(P0, True)
+    for x in range(16):
+        out_p[x] = KEEP * P0[x + 1, 8:24] + wgt[x] * (src[x] + off_diagonal(P0, x))
+
     out_f[...] = frac_now + frac_step * (
-        fsrc[...] + couple * pressure_at + peers - frac_diag * frac_now
+        fsrc[...] + couple * (pressure_at + prolong_at_slots(nodes)) + peers - frac_diag * frac_now
     )
 
-    for kind in range(3):
+    for kind in range(2):
         for i in range(8):
 
             @pl.when(is_there(AROUND[i]))
@@ -575,25 +621,28 @@
 
     def local(src, acc, fac, bas, cd, cr, fs, fa, fl, ft, fc, fp, cnt):
         row = lambda v: v.reshape(1, v.shape[0])
-        operands = (src, acc, fac, bas, cd, cr, row(fs), row(fa), row(fl), ft, row(fc), fp, row(cnt))
+        operands = (src, acc, fac, bas, cd, cr, row(fs), row(fa), row(fl), ft, row(fc), fp, cnt)
         vmem = pltpu.VMEM
         pressure, fracture = pl.pallas_call(
             lambda *refs: kernel(n_blk, n_lay, *refs),
             out_shape=(
-                jax.ShapeDtypeStruct((CX, CY, CZ), F32),
-                jax.ShapeDtypeStruct((1, FS), F32),
+                vmem((CX, CY, CZ), F32),
+                vmem((1, FS), F32),
             ),
-            in_specs=[pl.BlockSpec(memory_space=pl.ANY)] * 13,
+            in_specs=[pl.BlockSpec(memory_space=pltpu.HBM)] * 12 + [pl.BlockSpec(memory_space=pltpu.SMEM)],
             out_specs=[pl.BlockSpec(memory_space=vmem)] * 2,
-            scratch_shapes=[vmem(v.shape, v.dtype) for v in operands]
+            scratch_shapes=[vmem(v.shape, v.dtype) for v in operands[:-1]]
+            + [pltpu.SMEM((1,), I32)]
             + [
                 vmem((CX + 2, 32, CZ), F32),
                 vmem((CX + 2, 32, CZ), F32),
                 vmem((CX, CY, CZ), F32),
                 vmem((CZ, FS), BF16),
+                vmem((2, LANES, FS), BF16),
+                vmem((2, 8, FS), F32),
                 vmem((5, 8, LANES), F32),
-                vmem((3, 8, LANES), F32),
-                vmem((3, 8, 8, LANES), F32),
+                vmem((2, 8, LANES), F32),
+                vmem((2, 8, 8, LANES), F32),
                 vmem((2, 4, CY, CZ), F32),
                 vmem((2, 4, CX, CZ), F32),
                 vmem((2, 4, CX, CZ), F32),
@@ -603,8 +652,8 @@
                 vmem((4, LANES), F32),
                 vmem((2, 4, LANES), F32),
                 pltpu.SemaphoreType.DMA((13,)),
-                pltpu.SemaphoreType.DMA((3, 8)),
-                pltpu.SemaphoreType.DMA((3, 8)),
+                pltpu.SemaphoreType.DMA((2, 8)),
+                pltpu.SemaphoreType.DMA((2, 8)),
                 pltpu.SemaphoreType.DMA((2, 2)),
                 pltpu.SemaphoreType.DMA((2, 2)),
                 pltpu.SemaphoreType.DMA((2, 2)),

time: 30.1 us -> 25.7 us (0.85)
  Pallas kernels: 25.7 us -> 22.9 us
  local copies, waits for them, and re-layouts: 2.92 us -> 1.28 us
    pallas_call x1, Pallas kernels: 25.7 us -> 22.9 us  [local(): pl.pallas_call(lambda *refs: kernel(n_blk, n_lay, *refs), out_shape=(vmem...]
    unnamed x2, local copies, waits for them, and re-layouts: 2.92 us -> 1.28 us
where the time goes in v2:
time: 25.7 us; the launch traced here: 25.5 us
  Pallas kernels  22.9 us (89%)
  between operations  1.29 us (5%)
  local copies, waits for them, and re-layouts  1.28 us (5%)
    pallas_call x1, Pallas kernels, local(): pl.pallas_call(lambda *refs: kernel(n_blk, n_lay, *refs), out_shape=(vmem...  22.9 us
    unnamed x2, local copies, waits for them, and re-layouts  1.28 us

profile of v2, /device:TPU:33, one launch (start us, length us, event | category | flops | bytes accessed | tf_op | source)
XLA Modules:
  0.0 25.5 jit_solution(3669237542509106713)
XLA Ops:
  1.3 22.9 %shard_map.140 = (f32[16,16,256]{2,1,0:T(8,128)S(1)}, f32[1,512]{1,0:T(1,128)S(1)}) custom-call(f32[16,16,256]{2,1,0:T(8,128)} %refs_0_.1, f32[16,16,256]{2,1,0:T(8,128)} %refs_1_.1, f32[6,16,16,256]{3,2,1,0:T(8,128)} %refs_2_.1, f32[4,16,16,256]{3,2,1,0:T(8,128)} %refs_3_.1, f32[4,4]{1,0:T(4,128)} %refs_4_.1, f32[4,4,4]{2,1,0:T(4,128)} %refs_5_.1, ...), custom_call_target="tpu_custom_call" | custom-call | tf_op jit(solution)/shard_map/pallas_call | solution.py:626
  24.2 0.7 %copy.17 = f32[16,16,256]{2,1,0:T(8,128)} copy(f32[16,16,256]{2,1,0:T(8,128)S(1)} %get-tuple-element.6) | data formatting | bytes 524288
  24.9 0.6 %copy.18 = f32[512]{0:T(512)} copy(f32[512]{0:T(512)S(1)} %bitcast.5) | data formatting | bytes 4096

commit v3 on v2

--- a/solution.py
+++ b/solution.py
@@ -19,6 +19,7 @@
 LANES = 128
 
 AROUND = ((-1, -1), (-1, 0), (-1, 1), (0, -1), (0, 1), (1, -1), (1, 0), (1, 1))
+ORDER = (2, 7, 4, 0, 5, 3, 1, 6)
 
 
 def iota(shape, dim):
@@ -86,23 +87,14 @@
     ctile,
     snd,
     rcv,
-    bxh,
-    byh,
+    bh,
     bys,
-    pxh,
-    pyh,
+    ph,
     pys,
     fsnd,
     frcv,
     load_sem,
-    tile_ssem,
-    tile_rsem,
-    basis_ssem,
-    basis_rsem,
-    edge_ssem,
-    edge_rsem,
-    frac_ssem,
-    frac_rsem,
+    sems,
 ):
     b = lax.axis_index("blk")
     l = lax.axis_index("lay")
@@ -119,6 +111,19 @@
     has_prev = position > 0
     next_dev = ((position + 1) // n_lay, lax.rem(position + 1, n_lay))
     prev_dev = ((position - 1) // n_lay, lax.rem(position - 1 + n_lay, n_lay))
+
+    n_i = (l > 0).astype(I32) + (l < n_lay - 1).astype(I32)
+    n_j = (b > 0).astype(I32) + (b < n_blk - 1).astype(I32)
+    n_sides = n_i + n_j
+    n_around = n_sides + n_i * n_j
+    n_owners = has_prev.astype(I32) + has_next.astype(I32)
+
+    def wait_all(n, most, block, sem):
+        for m in range(1, most + 1):
+
+            @pl.when(n == m)
+            def _():
+                pltpu.make_async_copy(block.at[0:m], block.at[0:m], sem).wait()
 
     loads = []
     for i, (hbm, vmem) in enumerate(
@@ -144,7 +149,8 @@
 
     barrier = pltpu.get_barrier_semaphore()
     count = jnp.int32(0)
-    for step in AROUND:
+    for i in ORDER:
+        step = AROUND[i]
         there = is_there(step)
         count = count + there.astype(I32)
 
@@ -182,13 +188,13 @@
 
         @pl.when(jnp.logical_not(is_there(step_x)))
         def _():
-            bxh[s] = jnp.zeros((4, CY, CZ), F32)
-            pxh[s] = jnp.zeros((CY, CZ), F32)
+            bh[2 + s] = jnp.zeros((4, CY, CZ), F32)
+            ph[2 + s] = jnp.zeros((CY, CZ), F32)
 
         @pl.when(jnp.logical_not(is_there(step_y)))
         def _():
-            byh[s] = jnp.zeros((4, CX, CZ), F32)
-            pyh[s] = jnp.zeros((CX, CZ), F32)
+            bh[s] = jnp.zeros((4, CX, CZ), F32)
+            ph[s] = jnp.zeros((CX, CZ), F32)
 
     loads[2].wait()
     loads[3].wait()
@@ -210,54 +216,39 @@
         return pltpu.make_async_remote_copy(
             src_ref=snd.at[kind],
             dst_ref=rcv.at[kind, 7 - i],
-            send_sem=tile_ssem.at[kind, i],
-            recv_sem=tile_rsem.at[kind, 7 - i],
+            send_sem=sems.at[0],
+            recv_sem=sems.at[1 + kind],
             device_id=device(AROUND[i]),
             device_id_type=MESH,
         )
 
-    def tile_arrival(kind, i):
-        return pltpu.make_async_remote_copy(
-            src_ref=snd.at[kind],
-            dst_ref=rcv.at[kind, i],
-            send_sem=tile_ssem.at[kind, i],
-            recv_sem=tile_rsem.at[kind, i],
-            device_id=device(AROUND[i]),
-            device_id_type=MESH,
-        )
-
     def send_tile(kind):
-        for i in range(8):
+        for i in ORDER:
 
             @pl.when(is_there(AROUND[i]))
             def _():
                 tile_copy(kind, i).start()
 
     def await_tile(kind):
-        for i in range(8):
-
-            @pl.when(is_there(AROUND[i]))
-            def _():
-                tile_arrival(kind, i).wait_recv()
-
-    def side_copy(source, target, ssem, rsem, axis, s, arrival=False):
-        slot = s if arrival else 1 - s
+        wait_all(n_around, 8, rcv.at[kind], sems.at[1 + kind])
+
+    def side_copy(source, target, ssem, rsem, axis, s):
         return pltpu.make_async_remote_copy(
             src_ref=source,
-            dst_ref=target.at[slot],
-            send_sem=ssem.at[axis, s],
-            recv_sem=rsem.at[axis, slot],
+            dst_ref=target.at[2 * axis + 1 - s],
+            send_sem=ssem,
+            recv_sem=rsem,
             device_id=device(AROUND[sides[axis][s]]),
             device_id_type=MESH,
         )
 
-    def basis_copy(axis, s, arrival=False):
+    def basis_copy(axis, s):
         source = bas.at[:, 15 * s] if axis else bys.at[s]
-        return side_copy(source, bxh if axis else byh, basis_ssem, basis_rsem, axis, s, arrival)
-
-    def edge_copy(axis, s, arrival=False):
+        return side_copy(source, bh, sems.at[3], sems.at[4], axis, s)
+
+    def edge_copy(axis, s):
         source = P1.at[16 if s else 1, 8:24] if axis else pys.at[s]
-        return side_copy(source, pxh if axis else pyh, edge_ssem, edge_rsem, axis, s, arrival)
+        return side_copy(source, ph, sems.at[3], sems.at[5], axis, s)
 
     def on_sides(make, axis, act):
         for s in range(2):
@@ -304,14 +295,14 @@
         for s, plane in enumerate(x_planes):
             rc, rs = (5, 4) if s else (0, 1)
             for k, (into, r) in enumerate(((centre, rc), (centre, rs), (beside, rc), (beside, rs))):
-                add(into, r, fold(bxh[s, k] * plane))
+                add(into, r, fold(bh[2 + s, k] * plane))
         tile = jnp.zeros((8, LANES), F32)
         y_c = jnp.zeros((16, LANES), F32)
         y_s = jnp.zeros((16, LANES), F32)
         for s, plane in enumerate(y_planes):
             near, far = (5, 6) if s else (2, 1)
             for k in range(4):
-                value = lane_sum(fold(byh[s, k] * plane))
+                value = lane_sum(fold(bh[s, k] * plane))
                 placed = jnp.where(lane16 == (far if k < 2 else near), value, 0.0)
                 if k % 2 == 0:
                     y_c = y_c + placed
@@ -370,10 +361,10 @@
     def prolong_x_plane(s, centre, beside):
         rc, rs = (5, 4) if s else (0, 1)
         return (
-            bxh[s, 0] * centre[rc]
-            + bxh[s, 1] * centre[rs]
-            + bxh[s, 2] * beside[rc]
-            + bxh[s, 3] * beside[rs]
+            bh[2 + s, 0] * centre[rc]
+            + bh[2 + s, 1] * centre[rs]
+            + bh[2 + s, 2] * beside[rc]
+            + bh[2 + s, 3] * beside[rs]
         )
 
     def prolong_y_plane(s, nodes):
@@ -384,10 +375,10 @@
             return lane_sum(jnp.where(lane16 == lane, value, 0.0))
 
         return (
-            byh[s, 0] * pick(centre, far)
-            + byh[s, 1] * pick(beside, far)
-            + byh[s, 2] * pick(centre, near)
-            + byh[s, 3] * pick(beside, near)
+            bh[s, 0] * pick(centre, far)
+            + bh[s, 1] * pick(beside, far)
+            + bh[s, 2] * pick(centre, near)
+            + bh[s, 3] * pick(beside, near)
         )
 
     loads[0].wait()
@@ -521,13 +512,12 @@
     for t in range(4):
         fsnd[t : t + 1, :] = frac_now[:, LANES * t : LANES * t + LANES]
 
-    def frac_copy(s, arrival=False):
-        slot = s if arrival else 1 - s
+    def frac_copy(s):
         return pltpu.make_async_remote_copy(
             src_ref=fsnd,
-            dst_ref=frcv.at[slot],
-            send_sem=frac_ssem.at[s],
-            recv_sem=frac_rsem.at[slot],
+            dst_ref=frcv.at[1 - s],
+            send_sem=sems.at[6],
+            recv_sem=sems.at[7],
             device_id=next_dev if s else prev_dev,
             device_id_type=MESH,
         )
@@ -541,22 +531,22 @@
 
     on_owners(lambda s: frac_copy(s).start())
 
-    on_sides(lambda axis, s: basis_copy(axis, s, True), 1, lambda copy: copy.wait_recv())
-    on_sides(lambda axis, s: basis_copy(axis, s, True), 0, lambda copy: copy.wait_recv())
+    wait_all(n_sides, 4, bh, sems.at[4])
 
     def set_rims(p, earlier):
         for s in range(2):
             plane = prolong_x_plane(s, centre, beside)
-            p[17 if s else 0, 8:24] = plane + pxh[s] if earlier else plane
+            p[17 if s else 0, 8:24] = plane + ph[2 + s] if earlier else plane
             plane = prolong_y_plane(s, nodes)
             if earlier:
-                plane = plane + pyh[s]
+                plane = plane + ph[s]
             for x in range(16):
                 p[x + 1, 24 if s else 7, :] = plane[x]
 
     set_rims(P0, False)
     for x in range(16):
         P1[x + 1, 8:24] = KEEP * P0[x + 1, 8:24] + wgt[x] * (src[x] + off_diagonal(P0, x))
+    wait_all(n_sides, 4, bh, sems.at[3])
     on_sides(edge_copy, 1, lambda copy: copy.start())
     for s in range(2):
         pys[s] = pack_rows(lambda x: P1[x + 1, 8 + 15 * s : 9 + 15 * s, :])
@@ -568,6 +558,7 @@
         (edge_face[0] * pys[0], edge_face[1] * pys[1]),
     )
     snd[1] = own_part
+    wait_all(n_around, 8, rcv.at[0], sems.at[0])
     send_tile(1)
 
     def put_source(i, found):
@@ -576,7 +567,7 @@
 
     scatter(couple * frac_now, put_source)
     pressure_at = gather(lambda i: own_rows(P1, i))
-    on_owners(lambda s: frac_copy(s, True).wait_recv())
+    wait_all(n_owners, 2, frcv, sems.at[7])
     table = jnp.concatenate([frcv[0], fsnd[...], frcv[1], jnp.zeros((4, LANES), F32)], axis=0)
     high, low = split(table)
     peers = jnp.zeros((1, FS), F32)
@@ -593,8 +584,7 @@
     centre, beside = fields(nodes)
     for x in range(16):
         P0[x + 1, 8:24] = P1[x + 1, 8:24] + prolong_row(x, centre, beside)
-    on_sides(lambda axis, s: edge_copy(axis, s, True), 1, lambda copy: copy.wait_recv())
-    on_sides(lambda axis, s: edge_copy(axis, s, True), 0, lambda copy: copy.wait_recv())
+    wait_all(n_sides, 4, ph, sems.at[5])
     set_rims(P0, True)
     for x in range(16):
         out_p[x] = KEEP * P0[x + 1, 8:24] + wgt[x] * (src[x] + off_diagonal(P0, x))
@@ -603,17 +593,20 @@
         fsrc[...] + couple * (pressure_at + prolong_at_slots(nodes)) + peers - frac_diag * frac_now
     )
 
-    for kind in range(2):
-        for i in range(8):
-
-            @pl.when(is_there(AROUND[i]))
-            def _():
-                tile_copy(kind, i).wait_send()
-
-    for axis in range(2):
-        on_sides(basis_copy, axis, lambda copy: copy.wait_send())
-        on_sides(edge_copy, axis, lambda copy: copy.wait_send())
-    on_owners(lambda s: frac_copy(s).wait_send())
+    wait_all(n_around, 8, rcv.at[1], sems.at[0])
+    wait_all(n_sides, 4, ph, sems.at[3])
+    wait_all(n_owners, 2, frcv, sems.at[6])
+
+
+def store(p_v, f_v, p_h, f_h, sem):
+    copies = [
+        pltpu.make_async_copy(p_v, p_h, sem.at[0]),
+        pltpu.make_async_copy(f_v, f_h, sem.at[1]),
+    ]
+    for copy in copies:
+        copy.start()
+    for copy in copies:
+        copy.wait()
 
 
 def solution(mesh):
@@ -643,26 +636,30 @@
                 vmem((5, 8, LANES), F32),
                 vmem((2, 8, LANES), F32),
                 vmem((2, 8, 8, LANES), F32),
-                vmem((2, 4, CY, CZ), F32),
+                vmem((4, 4, CX, CZ), F32),
                 vmem((2, 4, CX, CZ), F32),
-                vmem((2, 4, CX, CZ), F32),
-                vmem((2, CY, CZ), F32),
-                vmem((2, CX, CZ), F32),
+                vmem((4, CX, CZ), F32),
                 vmem((2, CX, CZ), F32),
                 vmem((4, LANES), F32),
                 vmem((2, 4, LANES), F32),
-                pltpu.SemaphoreType.DMA((13,)),
-                pltpu.SemaphoreType.DMA((2, 8)),
-                pltpu.SemaphoreType.DMA((2, 8)),
-                pltpu.SemaphoreType.DMA((2, 2)),
-                pltpu.SemaphoreType.DMA((2, 2)),
-                pltpu.SemaphoreType.DMA((2, 2)),
-                pltpu.SemaphoreType.DMA((2, 2)),
-                pltpu.SemaphoreType.DMA((2,)),
-                pltpu.SemaphoreType.DMA((2,)),
+                pltpu.SemaphoreType.DMA((12,)),
+                pltpu.SemaphoreType.DMA((8,)),
             ],
             compiler_params=pltpu.CompilerParams(collective_id=0, has_side_effects=True),
         )(*operands)
+        pressure, fracture = pl.pallas_call(
+            store,
+            out_shape=(
+                jax.ShapeDtypeStruct((CX, CY, CZ), F32),
+                jax.ShapeDtypeStruct((1, FS), F32),
+            ),
+            in_specs=[pl.BlockSpec(memory_space=vmem)] * 2,
+            out_specs=[pl.BlockSpec(memory_space=pltpu.HBM)] * 2,
+            scratch_shapes=[pltpu.SemaphoreType.DMA((2,))],
+        )(
+            pltpu.with_memory_space_constraint(pressure, vmem),
+            pltpu.with_memory_space_constraint(fracture, vmem),
+        )
         return pressure, fracture.reshape(FS)
 
     return jax.shard_map(

time: 25.7 us -> 24.4 us (0.949)
  the two profiles are of different devices: /device:TPU:33 before, /device:TPU:35 now
where the time goes in v3:
time: 24.4 us; the launch traced here: 24.3 us
  Pallas kernels  23 us (94%)
  between operations  1.29 us (5%)
    pallas_call x1, Pallas kernels, local(): pl.pallas_call(lambda *refs: kernel(n_blk, n_lay, *refs), out_shape=(vmem...  22.3 us
    pallas_call x1, Pallas kernels, local(): pl.pallas_call(store, out_shape=(jax.ShapeDtypeStruct((CX, CY, CZ), F32),...  0.72 us

profile of v3, /device:TPU:35, one launch (start us, length us, event | category | flops | bytes accessed | tf_op | source)
XLA Modules:
  0.0 24.3 jit_solution(3849659301331353470)
XLA Ops:
  1.3 22.3 %shard_map.140 = (f32[16,16,256]{2,1,0:T(8,128)S(1)}, f32[1,512]{1,0:T(1,128)S(1)}) custom-call(f32[16,16,256]{2,1,0:T(8,128)} %refs_0_.1, f32[16,16,256]{2,1,0:T(8,128)} %refs_1_.1, f32[6,16,16,256]{3,2,1,0:T(8,128)} %refs_2_.1, f32[4,16,16,256]{3,2,1,0:T(8,128)} %refs_3_.1, f32[4,4]{1,0:T(4,128)} %refs_4_.1, f32[4,4,4]{2,1,0:T(4,128)} %refs_5_.1, ...), custom_call_target="tpu_custom_call" | custom-call | tf_op jit(solution)/shard_map/pallas_call | solution.py:619
  23.6 0.7 %shard_map.141 = (f32[16,16,256]{2,1,0:T(8,128)}, f32[1,512]{1,0:T(1,128)}) custom-call(f32[16,16,256]{2,1,0:T(8,128)S(1)} %get-tuple-element.6.p_v, f32[1,512]{1,0:T(1,128)S(1)} %get-tuple-element.7.f_v), custom_call_target="tpu_custom_call" | custom-call | tf_op jit(solution)/shard_map/pallas_call | solution.py:650

commit v4 on v3

--- a/solution.py
+++ b/solution.py
@@ -17,6 +17,7 @@
 OMEGA = 0.8
 KEEP = 1.0 - OMEGA
 LANES = 128
+ROW = 8
 
 AROUND = ((-1, -1), (-1, 0), (-1, 1), (0, -1), (0, 1), (1, -1), (1, 0), (1, 1))
 ORDER = (2, 7, 4, 0, 5, 3, 1, 6)
@@ -93,6 +94,7 @@
     pys,
     fsnd,
     frcv,
+    fpass,
     load_sem,
     sems,
 ):
@@ -111,6 +113,12 @@
     has_prev = position > 0
     next_dev = ((position + 1) // n_lay, lax.rem(position + 1, n_lay))
     prev_dev = ((position - 1) // n_lay, lax.rem(position - 1 + n_lay, n_lay))
+
+    first = (lax.rem(b, ROW) == 0) & has_prev & (b > 0)
+    passes = first & (l == n_lay - 1)
+    asks = first & (l == 0)
+    sends_prev = has_prev & jnp.logical_not(asks)
+    from_next = has_next & jnp.logical_not((lax.rem(b, ROW) == ROW - 1) & (l == n_lay - 1))
 
     n_i = (l > 0).astype(I32) + (l < n_lay - 1).astype(I32)
     n_j = (b > 0).astype(I32) + (b < n_blk - 1).astype(I32)
@@ -158,8 +166,9 @@
         def _():
             pl.semaphore_signal(barrier, inc=1, device_id=device(step), device_id_type=MESH)
 
-    for there, dev in ((has_next, next_dev), (has_prev, prev_dev)):
+    for there in (has_next, sends_prev, asks):
         count = count + there.astype(I32)
+    for there, dev in ((from_next, next_dev), (has_prev, prev_dev), (passes, (b, 0))):
 
         @pl.when(there)
         def _():
@@ -244,7 +253,7 @@
 
     def basis_copy(axis, s):
         source = bas.at[:, 15 * s] if axis else bys.at[s]
-        return side_copy(source, bh, sems.at[3], sems.at[4], axis, s)
+        return side_copy(source, bh, sems.at[3], sems.at[4 if axis else 8], axis, s)
 
     def edge_copy(axis, s):
         source = P1.at[16 if s else 1, 8:24] if axis else pys.at[s]
@@ -390,7 +399,14 @@
             bys[s, k] = pack_rows(lambda x: bas[k, x, 15 * s : 15 * s + 1, :])
     pl.semaphore_wait(barrier, count)
     send_tile(0)
-    on_sides(basis_copy, 0, lambda copy: copy.start())
+    def send_y_basis(core):
+        for s in range(2):
+
+            @pl.when(is_there(AROUND[sides[0][s]]) & (lax.rem(l, 2) == core))
+            def _():
+                basis_copy(0, s).start()
+
+    send_y_basis(0)
     on_sides(basis_copy, 1, lambda copy: copy.start())
 
     for i in range(4, 12):
@@ -429,7 +445,11 @@
     slot_cols = node_of(slot_y)
     for i in range(2):
         chot[i] = (iota((LANES, FS), 0) == slot_cols[i]).astype(F32).astype(BF16)
-    at_slot = [gather(lambda i: bas[k, 4 * i : 4 * i + 4].reshape(64, CZ)) for k in range(4)]
+    at_slot = []
+    for k in range(4):
+        at_slot.append(gather(lambda i: bas[k, 4 * i : 4 * i + 4].reshape(64, CZ)))
+        if k == 1:
+            send_y_basis(1)
     sub_slot = iota((8, FS), 0)
     for i in range(2):
         near[i] = jnp.where(sub_slot == slot_rows[0], at_slot[2 * i], 0.0) + jnp.where(
@@ -464,6 +484,7 @@
     for x in range(16):
         fac[4, x] = jnp.where(lane_z == CZ - 1, 0.0, fac[4, x])
         fac[5, x] = jnp.where(lane_z == 0, 0.0, fac[5, x])
+    edge_wgt = [pack_rows(lambda x: wgt[x, 15 * s : 15 * s + 1, :]) for s in range(2)]
     edge_face = [
         pack_rows(lambda x: fac[3, x, 0:1, :]),
         pack_rows(lambda x: fac[2, x, 15:16, :]),
@@ -522,8 +543,28 @@
             device_id_type=MESH,
         )
 
+    def pass_in():
+        return pltpu.make_async_remote_copy(
+            src_ref=fsnd,
+            dst_ref=fpass,
+            send_sem=sems.at[6],
+            recv_sem=sems.at[9],
+            device_id=(b, n_lay - 1),
+            device_id_type=MESH,
+        )
+
+    def pass_out():
+        return pltpu.make_async_remote_copy(
+            src_ref=fpass,
+            dst_ref=frcv.at[1],
+            send_sem=sems.at[10],
+            recv_sem=sems.at[7],
+            device_id=(b - 1, l),
+            device_id_type=MESH,
+        )
+
     def on_owners(act):
-        for s, there in enumerate((has_prev, has_next)):
+        for s, there in enumerate((sends_prev, has_next)):
 
             @pl.when(there)
             def _():
@@ -531,25 +572,29 @@
 
     on_owners(lambda s: frac_copy(s).start())
 
-    wait_all(n_sides, 4, bh, sems.at[4])
-
-    def set_rims(p, earlier):
+    @pl.when(asks)
+    def _():
+        pass_in().start()
+
+    wait_all(n_i, 2, bh, sems.at[4])
+
+    def set_x_rims(p, earlier):
         for s in range(2):
             plane = prolong_x_plane(s, centre, beside)
             p[17 if s else 0, 8:24] = plane + ph[2 + s] if earlier else plane
-            plane = prolong_y_plane(s, nodes)
-            if earlier:
-                plane = plane + ph[s]
-            for x in range(16):
-                p[x + 1, 24 if s else 7, :] = plane[x]
-
-    set_rims(P0, False)
+
+    set_x_rims(P0, False)
     for x in range(16):
         P1[x + 1, 8:24] = KEEP * P0[x + 1, 8:24] + wgt[x] * (src[x] + off_diagonal(P0, x))
+    wait_all(n_j, 2, bh, sems.at[8])
+    for s in range(2):
+        edge = pack_rows(lambda x: P1[x + 1, 8 + 15 * s : 9 + 15 * s, :])
+        edge = edge + edge_wgt[s] * (edge_face[s] * prolong_y_plane(s, nodes))
+        pys[s] = edge
+        for x in range(16):
+            P1[x + 1, 8 + 15 * s, :] = edge[x]
     wait_all(n_sides, 4, bh, sems.at[3])
     on_sides(edge_copy, 1, lambda copy: copy.start())
-    for s in range(2):
-        pys[s] = pack_rows(lambda x: P1[x + 1, 8 + 15 * s : 9 + 15 * s, :])
     on_sides(edge_copy, 0, lambda copy: copy.start())
 
     own_part = restrict_from_slots(couple * frac_now) + restrict(
@@ -567,6 +612,12 @@
 
     scatter(couple * frac_now, put_source)
     pressure_at = gather(lambda i: own_rows(P1, i))
+
+    @pl.when(passes)
+    def _():
+        pass_in().wait_recv()
+        pass_out().start()
+
     wait_all(n_owners, 2, frcv, sems.at[7])
     table = jnp.concatenate([frcv[0], fsnd[...], frcv[1], jnp.zeros((4, LANES), F32)], axis=0)
     high, low = split(table)
@@ -585,7 +636,11 @@
     for x in range(16):
         P0[x + 1, 8:24] = P1[x + 1, 8:24] + prolong_row(x, centre, beside)
     wait_all(n_sides, 4, ph, sems.at[5])
-    set_rims(P0, True)
+    set_x_rims(P0, True)
+    for s in range(2):
+        plane = prolong_y_plane(s, nodes) + ph[s]
+        for x in range(16):
+            P0[x + 1, 24 if s else 7, :] = plane[x]
     for x in range(16):
         out_p[x] = KEEP * P0[x + 1, 8:24] + wgt[x] * (src[x] + off_diagonal(P0, x))
 
@@ -596,6 +651,10 @@
     wait_all(n_around, 8, rcv.at[1], sems.at[0])
     wait_all(n_sides, 4, ph, sems.at[3])
     wait_all(n_owners, 2, frcv, sems.at[6])
+
+    @pl.when(passes)
+    def _():
+        pass_out().wait_send()
 
 
 def store(p_v, f_v, p_h, f_h, sem):
@@ -642,8 +701,9 @@
                 vmem((2, CX, CZ), F32),
                 vmem((4, LANES), F32),
                 vmem((2, 4, LANES), F32),
+                vmem((4, LANES), F32),
                 pltpu.SemaphoreType.DMA((12,)),
-                pltpu.SemaphoreType.DMA((8,)),
+                pltpu.SemaphoreType.DMA((11,)),
             ],
             compiler_params=pltpu.CompilerParams(collective_id=0, has_side_effects=True),
         )(*operands)

time: 24.4 us -> 23.8 us (0.975)
  the two profiles are of different devices: /device:TPU:35 before, /device:TPU:33 now
where the time goes in v4:
time: 23.8 us; the launch traced here: 23.6 us
  Pallas kernels  22.4 us (94%)
  between operations  1.29 us (5%)
    pallas_call x1, Pallas kernels, local(): pl.pallas_call(lambda *refs: kernel(n_blk, n_lay, *refs), out_shape=(vmem...  21.6 us
    pallas_call x1, Pallas kernels, local(): pl.pallas_call(store, out_shape=(jax.ShapeDtypeStruct((CX, CY, CZ), F32),...  0.72 us

profile of v4, /device:TPU:33, one launch (start us, length us, event | category | flops | bytes accessed | tf_op | source)
XLA Modules:
  0.0 23.6 jit_solution(10476787153477588782)
XLA Ops:
  1.3 21.6 %shard_map.140 = (f32[16,16,256]{2,1,0:T(8,128)S(1)}, f32[1,512]{1,0:T(1,128)S(1)}) custom-call(f32[16,16,256]{2,1,0:T(8,128)} %refs_0_.1, f32[16,16,256]{2,1,0:T(8,128)} %refs_1_.1, f32[6,16,16,256]{3,2,1,0:T(8,128)} %refs_2_.1, f32[4,16,16,256]{3,2,1,0:T(8,128)} %refs_3_.1, f32[4,4]{1,0:T(4,128)} %refs_4_.1, f32[4,4,4]{2,1,0:T(4,128)} %refs_5_.1, ...), custom_call_target="tpu_custom_call" | custom-call | tf_op jit(solution)/shard_map/pallas_call | solution.py:678
  22.9 0.7 %shard_map.141 = (f32[16,16,256]{2,1,0:T(8,128)}, f32[1,512]{1,0:T(1,128)}) custom-call(f32[16,16,256]{2,1,0:T(8,128)S(1)} %get-tuple-element.6.p_v, f32[1,512]{1,0:T(1,128)S(1)} %get-tuple-element.7.f_v), custom_call_target="tpu_custom_call" | custom-call | tf_op jit(solution)/shard_map/pallas_call | solution.py:710

commit v5 on v4

--- a/solution.py
+++ b/solution.py
@@ -448,7 +448,7 @@
     at_slot = []
     for k in range(4):
         at_slot.append(gather(lambda i: bas[k, 4 * i : 4 * i + 4].reshape(64, CZ)))
-        if k == 1:
+        if k == 3:
             send_y_basis(1)
     sub_slot = iota((8, FS), 0)
     for i in range(2):
@@ -594,9 +594,6 @@
         for x in range(16):
             P1[x + 1, 8 + 15 * s, :] = edge[x]
     wait_all(n_sides, 4, bh, sems.at[3])
-    on_sides(edge_copy, 1, lambda copy: copy.start())
-    on_sides(edge_copy, 0, lambda copy: copy.start())
-
     own_part = restrict_from_slots(couple * frac_now) + restrict(
         lambda x: src[x] - acc[x] * P1[x + 1, 8:24] + off_diagonal(P1, x),
         (fac[1, 0] * P1[1, 8:24], fac[0, 15] * P1[16, 8:24]),
@@ -605,6 +602,9 @@
     snd[1] = own_part
     wait_all(n_around, 8, rcv.at[0], sems.at[0])
     send_tile(1)
+    on_sides(edge_copy, 1, lambda copy: copy.start())
+    on_sides(edge_copy, 0, lambda copy: copy.start())
+
 
     def put_source(i, found):
         for j in range(4):

time: 23.8 us -> 23.8 us (level)
  no operation moved by 1% of the time
where the time goes in v5:
time: 23.8 us; the launch traced here: 23.6 us
  Pallas kernels  22.3 us (94%)
  between operations  1.29 us (5%)
    pallas_call x1, Pallas kernels, local(): pl.pallas_call(lambda *refs: kernel(n_blk, n_lay, *refs), out_shape=(vmem...  21.6 us
    pallas_call x1, Pallas kernels, local(): pl.pallas_call(store, out_shape=(jax.ShapeDtypeStruct((CX, CY, CZ), F32),...  0.72 us

profile of v5, /device:TPU:33, one launch (start us, length us, event | category | flops | bytes accessed | tf_op | source)
XLA Modules:
  0.0 23.6 jit_solution(7057664022596854278)
XLA Ops:
  1.3 21.6 %shard_map.140 = (f32[16,16,256]{2,1,0:T(8,128)S(1)}, f32[1,512]{1,0:T(1,128)S(1)}) custom-call(f32[16,16,256]{2,1,0:T(8,128)} %refs_0_.1, f32[16,16,256]{2,1,0:T(8,128)} %refs_1_.1, f32[6,16,16,256]{3,2,1,0:T(8,128)} %refs_2_.1, f32[4,16,16,256]{3,2,1,0:T(8,128)} %refs_3_.1, f32[4,4]{1,0:T(4,128)} %refs_4_.1, f32[4,4,4]{2,1,0:T(4,128)} %refs_5_.1, ...), custom_call_target="tpu_custom_call" | custom-call | tf_op jit(solution)/shard_map/pallas_call | solution.py:678
  22.9 0.7 %shard_map.141 = (f32[16,16,256]{2,1,0:T(8,128)}, f32[1,512]{1,0:T(1,128)}) custom-call(f32[16,16,256]{2,1,0:T(8,128)S(1)} %get-tuple-element.6.p_v, f32[1,512]{1,0:T(1,128)S(1)} %get-tuple-element.7.f_v), custom_call_target="tpu_custom_call" | custom-call | tf_op jit(solution)/shard_map/pallas_call | solution.py:710
